TPU v7x, 32 devices: a whole 2x2x4 slice. The times are simulated.
32 devices in a mesh: dp: 4 (over y, x), row: 2 (over core), col: 4 (over z).
Axes of the slice: x: 2, y: 2, z: 4, core: 2. Of those that a mesh axis runs over, the one named last changes fastest.
Arguments:
- tokens: bfloat16 [4096, 2048], P('dp', ('row', 'col')), may hold values from -40 to 40
- gain_attn: float32 [2048], P(('row', 'col')), may hold values from 0.5 to 1.5
- gain_ffn: float32 [2048], P(('row', 'col')), may hold values from 0.5 to 1.5
- w_query: bfloat16 [2048, 2048], P('row', 'col'), may hold values from -0.125 to 0.125
- w_key: bfloat16 [2048, 2048], P('row', 'col'), may hold values from -0.125 to 0.125
- w_value: bfloat16 [2048, 2048], P('row', 'col'), may hold values from -0.125 to 0.125
- w_out: bfloat16 [2048, 2048], P('col', 'row'), may hold values from -1 to 1
- w_gate: bfloat16 [2048, 8192], P('row', 'col'), may hold values from -0.125 to 0.125
- w_up: bfloat16 [2048, 8192], P('row', 'col'), may hold values from -0.125 to 0.125
- w_down: bfloat16 [8192, 2048], P('col', 'row'), may hold values from -0.0625 to 0.0625
- grad_output: bfloat16 [4096, 2048], P('dp', ('row', 'col')), may hold values from -6 to 6
- segments: int32 [4, 1024], P('dp'), may hold values from 0 to 2, as said below
- positions: int32 [4, 1024], P('dp'), may hold values from 0 to 2047, as said below
Outputs:
- output: float32 [4096, 2048], P('dp', ('row', 'col'))
- grad_tokens: float32 [4096, 2048], P('dp', ('row', 'col'))
- grad_gain_attn: float32 [8, 4, 64], P(('row', 'col'), 'dp')
- grad_gain_ffn: float32 [8, 4, 64], P(('row', 'col'), 'dp')
- grad_w_query: float32 [2, 4, 256, 2048], P('row', 'dp', None, 'col')
- grad_w_key: float32 [2, 4, 256, 2048], P('row', 'dp', None, 'col')
- grad_w_value: float32 [2, 4, 256, 2048], P('row', 'dp', None, 'col')
- grad_w_out: float32 [4, 4, 128, 2048], P('col', 'dp', None, 'row')
- grad_w_gate: float32 [2, 4, 256, 8192], P('row', 'dp', None, 'col')
- grad_w_up: float32 [2, 4, 256, 8192], P('row', 'dp', None, 'col')
- grad_w_down: float32 [4, 4, 512, 2048], P('col', 'dp', None, 'row')
Inputs may be any that keep to these rules, and one draw needn't show every extreme that they name: `segments`: within a sequence the numbers never fall; each sequence holds three documents. `positions`: positions count up by one inside a document; the first document of a sequence starts at a position no larger than 2048 minus its length, the others at 0.
All inputs are finite; a program needn't handle non-finite values.
Results may differ from a plain program's by a relative error of at most 0.015.
Values may be sent and summed in bfloat16 or wider, within the bound.
A program may use at most 256 MiB of HBM per device.

v0:
```python
import functools

import jax
import jax.numpy as jnp
from jax import lax
from jax.experimental import pallas as pl
from jax.experimental.pallas import tpu as pltpu
from jax.sharding import PartitionSpec as P

MESH = pl.DeviceIdType.MESH
F32 = jnp.float32
BF16 = jnp.bfloat16
HD = 64
N_CHUNK = 4
norm_eps = 1e-05
rope_base = 130000.0
masked_score = -1e30
VMEM_LIMIT = 64 * 1024 * 1024 - 65536


def dot_nn(left, right):
    return lax.dot_general(left, right, (((1,), (0,)), ((), ())), preferred_element_type=F32)


def dot_nt(left, right):
    return lax.dot_general(left, right, (((1,), (1,)), ((), ())), preferred_element_type=F32)


def dot_tn(left, right):
    return lax.dot_general(left, right, (((0,), (0,)), ((), ())), preferred_element_type=F32)


def span(start, size):
    return pl.ds(pl.multiple_of(start, size), size)


def remote(src, dst, send_sem, recv_sem, where):
    return pltpu.make_async_remote_copy(
        src_ref=src,
        dst_ref=dst,
        send_sem=send_sem,
        recv_sem=recv_sem,
        device_id=where,
        device_id_type=MESH,
    )


def greet(peers):
    barrier = pltpu.get_barrier_semaphore()
    count = jnp.int32(0)
    for present, where in peers:

        @pl.when(present)
        def _():
            pl.semaphore_signal(barrier, inc=1, device_id=where, device_id_type=MESH)

        count = count + present.astype(jnp.int32)
    pl.semaphore_wait(barrier, count)


def line_peers(r, c, n_col):
    always = c >= 0
    return [
        (c > 0, {"col": jnp.maximum(c - 1, 0)}),
        (c < n_col - 1, {"col": jnp.minimum(c + 1, n_col - 1)}),
        (always, {"row": 1 - r}),
    ]


def group_peers(r, c, n_col):
    return [
        ((c != at) | (r != half), {"row": jnp.int32(half), "col": jnp.int32(at)})
        for half in range(2)
        for at in range(n_col)
    ]


class Gather:
    def __init__(self, full, send, recv, r, c, n_col, width, n_chunk=N_CHUNK):
        self.full, self.send, self.recv = full, send, recv
        self.r, self.c, self.n_col, self.width = r, c, n_col, width
        self.n_chunk = n_chunk

    def piece(self, half, at, chunk):
        cols = span(half * (self.n_col * self.width) + at * self.width, self.width)
        return self.full.at[chunk, :, cols]

    def copy(self, way, at, chunk):
        piece = self.piece(self.r, at, chunk)
        where = (
            {"col": jnp.maximum(self.c - 1, 0)},
            {"col": jnp.minimum(self.c + 1, self.n_col - 1)},
            {"row": 1 - self.r},
        )[way]
        return remote(
            piece, piece, self.send.at[way, at, chunk], self.recv.at[self.r, at, chunk], where
        )

    def wait(self, half, at, chunk):
        piece = self.piece(half, at, chunk)
        remote(
            piece, piece, self.send.at[0, at, chunk], self.recv.at[half, at, chunk], {"row": 1 - self.r}
        ).wait_recv()

    def start(self, chunk):
        c = self.c

        @pl.when(c > 0)
        def _():
            self.copy(0, c, chunk).start()

        @pl.when(c < self.n_col - 1)
        def _():
            self.copy(1, c, chunk).start()

        self.copy(2, c, chunk).start()

    def relay(self, distance, chunk):
        c, last = self.c, self.n_col - 1

        @pl.when(c + distance <= last)
        def _():
            at = c + distance
            self.wait(self.r, at, chunk)

            @pl.when(c > 0)
            def _():
                self.copy(0, at, chunk).start()

            self.copy(2, at, chunk).start()

        @pl.when(c - distance >= 0)
        def _():
            at = c - distance
            self.wait(self.r, at, chunk)

            @pl.when(c < last)
            def _():
                self.copy(1, at, chunk).start()

            self.copy(2, at, chunk).start()

    def tick(self, now):
        for distance in range(self.n_col - 1, 0, -1):
            chunk = now + 1 - distance

            @pl.when((chunk >= 0) & (chunk < self.n_chunk))
            def _():
                self.relay(distance, chunk)

    def wait_other(self, chunk):
        def one(at, carry):
            self.wait(1 - self.r, at, chunk)
            return carry

        lax.fori_loop(0, self.n_col, one, 0)

    def finish(self):
        c, last = self.c, self.n_col - 1

        def one(step, carry):
            at, chunk = step // self.n_chunk, step % self.n_chunk

            @pl.when((c > 0) & (at >= c))
            def _():
                self.copy(0, at, chunk).wait_send()

            @pl.when((c < last) & (at <= c))
            def _():
                self.copy(1, at, chunk).wait_send()

            self.copy(2, at, chunk).wait_send()
            return carry

        lax.fori_loop(0, self.n_col * self.n_chunk, one, 0)


class Scatter:
    def __init__(self, part, stage, inbox, send, recv, c, n_col, n_chunk=N_CHUNK):
        self.part, self.stage, self.inbox = part, stage, inbox
        self.send, self.recv, self.c, self.n_col = send, recv, c, n_col
        self.n_chunk = n_chunk
        self.width = stage.shape[-1]
        self.middle = (c > 0) & (c < n_col - 1)

    def term(self, chunk, dest):
        return self.part[chunk, :, span(dest * self.width, self.width)]

    def copy(self, way, chunk, dest):
        where = jnp.clip(self.c + 1 - 2 * way, 0, self.n_col - 1)
        return remote(
            self.stage.at[chunk, dest],
            self.inbox.at[way, chunk, dest],
            self.send.at[chunk, dest],
            self.recv.at[way, chunk, dest],
            {"col": where},
        )

    def open(self, chunk):
        @pl.when(jnp.logical_not(self.middle))
        def _():
            way = (self.c > 0).astype(jnp.int32)

            def ship(step, carry):
                dest = jnp.where(way == 0, self.n_col - 1 - step, step)
                self.stage[chunk, dest] = self.term(chunk, dest).astype(BF16)
                self.copy(way, chunk, dest).start()
                return carry

            lax.fori_loop(0, self.n_col - 1, ship, 0)

    def pass_on(self, way, chunk, dest):
        copy = self.copy(way, chunk, dest)
        copy.wait_recv()
        total = self.term(chunk, dest) + self.inbox[way, chunk, dest].astype(F32)
        self.stage[chunk, dest] = total.astype(BF16)
        copy.start()

    def near(self, chunk):
        @pl.when(self.middle)
        def _():
            way = (self.c > 1).astype(jnp.int32)

            def step_on(step, carry):
                self.pass_on(way, chunk, jnp.where(way == 0, self.n_col - 1 - step, step))
                return carry

            lax.fori_loop(0, 2, step_on, 0)

    def far(self, chunk):
        @pl.when(self.middle)
        def _():
            way = (self.c == 1).astype(jnp.int32)
            self.pass_on(way, chunk, jnp.where(self.c == 1, 0, self.n_col - 1))

    def total(self, chunk, out, at):
        c = self.c
        way = (c == 0).astype(jnp.int32)
        self.copy(way, chunk, c).wait_recv()
        out[at, :] = self.term(chunk, c) + self.inbox[way, chunk, c].astype(F32)

        @pl.when(self.middle)
        def _():
            self.copy(1, chunk, c).wait_recv()
            out[at, :] += self.inbox[1, chunk, c].astype(F32)

    def finish(self):
        def one(step, carry):
            chunk, dest = step // self.n_col, step % self.n_col

            @pl.when(dest != self.c)
            def _():
                self.copy(0, chunk, dest).wait_send()

            return carry

        lax.fori_loop(0, self.n_chunk * self.n_col, one, 0)

    @staticmethod
    def scratch(n_col, rows, width, n_chunk=N_CHUNK):
        return [
            pltpu.VMEM((n_chunk, rows, n_col * width), F32),
            pltpu.VMEM((n_chunk, n_col, rows, width), BF16),
            pltpu.VMEM((2, n_chunk, n_col, rows, width), BF16),
            pltpu.SemaphoreType.DMA((n_chunk, n_col)),
            pltpu.SemaphoreType.DMA((2, n_chunk, n_col)),
        ]


def gather_sems(n_col, n_chunk=N_CHUNK):
    return [
        pltpu.SemaphoreType.DMA((3, n_col, n_chunk)),
        pltpu.SemaphoreType.DMA((2, n_col, n_chunk)),
    ]


N_NOTE = 16


def put_notes(full, chunk, cols, values):
    rows = full.shape[1] - N_NOTE
    width = values[0].shape[1]
    at = lax.broadcasted_iota(jnp.int32, (N_NOTE, width), 0)
    notes = jnp.zeros((N_NOTE, width), F32)
    for n, value in enumerate(values):
        for piece in range(3):
            rounded = value.astype(BF16).astype(F32)
            notes = jnp.where(at == 3 * n + piece, rounded, notes)
            value = value - rounded
    full[chunk, rows:, cols] = notes.astype(BF16)


def get_note(full, chunk, cols, n):
    rows = full.shape[1] - N_NOTE
    notes = full[chunk, rows:, cols].astype(F32)
    return (notes[3 * n : 3 * n + 1, :] + notes[3 * n + 1 : 3 * n + 2, :]) + notes[3 * n + 2 : 3 * n + 3, :]


def as_row(column):
    return jnp.broadcast_to(column, (column.shape[0], 128)).T[0:1, :]


def as_column(row):
    return jnp.broadcast_to(row, (128, row.shape[1])).T[:, 0:1]


class Totals:
    def __init__(self, held, sent, inbox, send, recv, r, c):
        self.held, self.sent, self.inbox, self.send, self.recv = held, sent, inbox, send, recv
        self.partners = ({"row": 1 - r}, {"col": c + 1 - 2 * (c % 2)}, {"col": c + 2 - 4 * (c // 2)})

    def note(self, chunk, column):
        self.held[pl.ds(chunk, 1), :] = as_row(column)

    def copy(self, step):
        return remote(
            self.sent.at[step], self.inbox.at[step], self.send.at[step], self.recv.at[step], self.partners[step]
        )

    def exchange(self):
        for step in range(3):
            self.sent[step] = self.held[...]
            copy = self.copy(step)
            copy.start()
            copy.wait_recv()
            self.held[...] += self.inbox[step]

    def column(self, chunk):
        return as_column(self.held[pl.ds(chunk, 1), :])

    def finish(self):
        for step in range(3):
            self.copy(step).wait_send()

    @staticmethod
    def scratch(rows):
        return [
            pltpu.VMEM((8, rows), F32),
            pltpu.VMEM((3, 8, rows), F32),
            pltpu.VMEM((3, 8, rows), F32),
            pltpu.SemaphoreType.DMA((3,)),
            pltpu.SemaphoreType.DMA((3,)),
        ]


def lanes(shape):
    return lax.broadcasted_iota(jnp.int32, shape, len(shape) - 1)


def swap_halves(values):
    half, width = HD // 2, values.shape[-1]
    low = (lanes(values.shape) & (HD - 1)) < half
    return jnp.where(
        low, pltpu.roll(values, width - half, 1), pltpu.roll(values, half, 1)
    )


def widen(table, width):
    return jnp.concatenate([table] * (width // table.shape[-1]), axis=-1)


class Flush:
    def __init__(self, pairs, sems, rows):
        self.pairs, self.sems, self.rows = pairs, sems, rows

    def copy(self, n, chunk):
        source, target = self.pairs[n]
        at = span(chunk * self.rows, self.rows)
        if isinstance(source, tuple):
            source = source[0].at[chunk, 0 : self.rows, source[1]]
        else:
            source = source.at[at, :]
        return pltpu.make_async_copy(source, target.at[at, :], self.sems.at[n, chunk])

    def start(self, chunk, which=None):
        for n in range(len(self.pairs)) if which is None else which:
            self.copy(n, chunk).start()

    def finish(self):
        def one(chunk, carry):
            for n in range(len(self.pairs)):
                self.copy(n, chunk).wait()
            return carry

        lax.fori_loop(0, N_CHUNK, one, 0)


def fetches(pairs, sems):
    copies = [pltpu.make_async_copy(source, target, sems.at[n]) for n, (source, target) in enumerate(pairs)]
    for copy in copies:
        copy.start()
    return copies


def vmem():
    return pl.BlockSpec(memory_space=pltpu.VMEM)


def anywhere():
    return pl.BlockSpec(memory_space=pl.ANY)


def kernel_call(body, name, ident, outs, out_any, in_specs, scratch, flops):
    return pl.pallas_call(
        body,
        out_shape=outs,
        in_specs=in_specs,
        out_specs=[anywhere() if flag else vmem() for flag in out_any],
        scratch_shapes=scratch,
        compiler_params=pltpu.CompilerParams(
            collective_id=ident, has_side_effects=True, vmem_limit_bytes=VMEM_LIMIT
        ),
        cost_estimate=pl.CostEstimate(flops=flops, bytes_accessed=1 << 24, transcendentals=0),
        name=name,
    )


def project_kernel(
    n_col,
    x, gain, positions, segments, rope, dy, wq, wk, wv, wo, wg, wu, wd,
    q_out, k_out, v_out, h1_out, r1, cos_table, sin_table, seg_col, dy_end, dy_mid,
    wo_other, wg_other, wu_other, wd_other,
    full, hidden, weights, q, k, v, h1, ag_send, ag_recv,
    w_send, w_recv, d_send, d_recv, local, flushed,
):
    r, c = lax.axis_index("row"), lax.axis_index("col")
    tok, width = x.shape
    half = n_col * width
    heads = wq.shape[1] // 2
    units = wg.shape[1] // 2
    me = r * n_col + c
    rows = tok // N_CHUNK
    held = fetches(
        [
            (
                w.at[:, span(r * heads, heads)],
                weights.at[span(r * half, half), pl.ds(n * heads, heads)],
            )
            for n, w in enumerate((wq, wk, wv))
        ],
        local,
    )
    mine = span(me * width, width)
    for chunk in range(N_CHUNK):
        values = x[chunk * rows : (chunk + 1) * rows, :]
        full[chunk, 0:rows, mine] = values
        values = values.astype(F32)
        square = as_row(jnp.sum(values * values, axis=1, keepdims=True))
        put_notes(full, chunk, mine, (square, gain[...]))
    greet(group_peers(r, c, n_col))
    gather = Gather(full, ag_send, ag_recv, r, c, n_col, width)
    flush = Flush(((q, q_out), (k, k_out), (v, v_out), (h1, h1_out)), flushed, rows)

    def chunk_rows(chunk):
        return span(chunk * rows, rows)

    gather.start(0)
    gather.start(1)
    other = {"row": 1 - r}
    moved = [
        remote(
            w.at[:, span((1 - r) * heads, heads)],
            weights.at[span(r * half, half), pl.ds(n * heads, heads)],
            w_send.at[n], w_recv.at[n], other,
        )
        for n, w in enumerate((wq, wk, wv))
    ]
    moved.append(remote(wo.at[span((1 - r) * heads, heads), :], wo_other, w_send.at[3], w_recv.at[3], other))
    moved.append(remote(wg.at[:, span((1 - r) * units, units)], wg_other, w_send.at[4], w_recv.at[4], other))
    moved.append(remote(wu.at[:, span((1 - r) * units, units)], wu_other, w_send.at[5], w_recv.at[5], other))
    moved.append(remote(wd.at[span((1 - r) * units, units), :], wd_other, w_send.at[6], w_recv.at[6], other))
    inward = {"col": jnp.where(c == 0, 1, jnp.where(c == 1, 2, jnp.where(c == 2, 1, 2)))}
    at_end = (c == 0) | (c == 3)
    early_end = remote(dy, dy_end, d_send.at[0], d_recv.at[0], inward)
    early_mid = remote(dy, dy_mid, d_send.at[0], d_recv.at[1], inward)

    for copy in moved[:3]:
        copy.start()
    gather.tick(0)
    gather.start(2)
    for copy in moved[3:]:
        copy.start()

    def tables(chunk, carry):
        at = chunk_rows(chunk)
        place = jnp.broadcast_to(positions[:, at].astype(F32), (128, rows)).T
        angles = place * rope[0:1, :]
        cos_table[at, :] = jnp.cos(angles)
        sin_table[at, :] = jnp.sin(angles) * rope[1:2, :]
        seg_col[at, :] = jnp.broadcast_to(segments[:, at].astype(F32), (128, rows)).T
        return carry

    lax.fori_loop(0, N_CHUNK, tables, 0)
    gather.tick(1)
    gather.start(3)
    pl.when(at_end)(early_end.start)
    gather.tick(2)

    def compute(chunk):
        at = chunk_rows(chunk)
        square = jnp.zeros((1, rows), F32)
        for block in range(2 * n_col):
            square = square + get_note(full, chunk, pl.ds(block * width, width), 0)
        scale = lax.rsqrt(as_column(square) * (1.0 / (2 * half)) + norm_eps)
        r1[at, :] = jnp.broadcast_to(scale, (rows, r1.shape[1]))
        for block in range(2 * n_col):
            cols = pl.ds(block * width, width)
            values = full[chunk, 0:rows, cols].astype(F32)
            hidden[:, cols] = (values * scale * get_note(full, chunk, cols, 1)).astype(BF16)
        h1[at, :] = hidden[:, span(r * half, half)]
        values = dot_nn(hidden[...], weights[...])
        cos_rows = widen(cos_table[at, :], heads)
        sin_rows = widen(sin_table[at, :], heads)
        for n, out in enumerate((q, k)):
            part = values[:, n * heads : (n + 1) * heads]
            out[at, :] = (part * cos_rows + swap_halves(part) * sin_rows).astype(BF16)
        v[at, :] = values[:, 2 * heads :].astype(BF16)
        flush.start(chunk)

    for copy in held:
        copy.wait()
    for copy in moved[:3]:
        copy.wait_recv()

    def step(chunk, carry):
        gather.wait_other(chunk)
        compute(chunk)
        gather.tick(chunk + 3)
        pl.when((chunk == 0) & jnp.logical_not(at_end))(early_mid.start)
        return carry

    lax.fori_loop(0, N_CHUNK, step, 0)
    gather.finish()
    for copy in moved[3:]:
        copy.wait_recv()
    for copy in moved:
        copy.wait_send()
    early_end.wait_send()

    @pl.when(jnp.logical_not(at_end))
    def _():
        early_end.wait_recv()
        early_mid.wait_recv()

    flush.finish()


def project(n_col, x, gain, positions, segments, dy, wq, wk, wv, wo, wg, wu, wd):
    tok, width = x.shape
    full = 2 * n_col * width
    half = n_col * width
    heads, units = wq.shape[1] // 2, wg.shape[1] // 2
    lane = jnp.arange(128) % HD
    inv_freq = rope_base ** (-2.0 * (lane % (HD // 2)).astype(F32) / HD)
    rope = jnp.stack([inv_freq, jnp.where(lane < HD // 2, -1.0, 1.0)])
    shape = jax.ShapeDtypeStruct
    outs = [
        shape((tok, heads), BF16), shape((tok, heads), BF16), shape((tok, heads), BF16),
        shape((tok, half), BF16), shape((tok, 128), F32),
        shape((tok, 128), F32), shape((tok, 128), F32), shape((tok, 128), F32),
        shape((tok, width), BF16), shape((tok, width), BF16),
        shape((heads, wo.shape[1]), BF16), shape((half, units), BF16),
        shape((half, units), BF16), shape((units, wd.shape[1]), BF16),
    ]
    scratch = [
        pltpu.VMEM((N_CHUNK, tok // N_CHUNK + N_NOTE, full), BF16),
        pltpu.VMEM((tok // N_CHUNK, full), BF16),
        pltpu.VMEM((full, 3 * heads), BF16),
        *[pltpu.VMEM((tok, heads), BF16)] * 3,
        pltpu.VMEM((tok, half), BF16),
        *gather_sems(n_col),
        pltpu.SemaphoreType.DMA((7,)),
        pltpu.SemaphoreType.DMA((7,)),
        pltpu.SemaphoreType.DMA((1,)),
        pltpu.SemaphoreType.DMA((2,)),
        pltpu.SemaphoreType.DMA((3,)),
        pltpu.SemaphoreType.DMA((4, N_CHUNK)),
    ]
    return kernel_call(
        functools.partial(project_kernel, n_col), "project", 1, outs,
        [True] * 4 + [False] * 4 + [True] * 6,
        [vmem()] * 5 + [anywhere()] * 8, scratch, 6 * tok * full * heads,
    )(x, gain, positions, segments, rope, dy, wq, wk, wv, wo, wg, wu, wd)


def allowed_pairs(seg_col, seg_row, chunk, rows, keys):
    seg_row = seg_row.astype(F32)
    query_at = chunk * rows + lax.broadcasted_iota(jnp.int32, (rows, keys), 0)
    key_at = lanes((rows, keys))
    return (key_at <= query_at) & (seg_col[:, 0:1] == seg_row)


def of_head(values, head):
    return jnp.where((lanes(values.shape) // HD) == head, values, jnp.zeros_like(values))


class LateGather:
    def __init__(self, full, send, recv, r, c, n_col, width):
        self.inner = Gather(full, send, recv, r, c, n_col, width)
        self.c = c
        self.end = (c == 0) | (c == 3)
        self.near_end = jnp.where(c < 2, 0, 3)
        self.far_end = 3 - self.near_end
        self.other = 3 - c
        self.outward = (c >= 2).astype(jnp.int32)

    def copy(self, way, at, chunk):
        piece = self.inner.piece(self.inner.r, at, chunk)
        where = ({"col": self.near_end}, {"col": self.other}, {"row": 1 - self.inner.r})[way]
        return remote(
            piece, piece, self.inner.send.at[way, at, chunk], self.inner.recv.at[self.inner.r, at, chunk], where
        )

    def start(self):
        c = self.c

        def one(chunk, carry):
            self.copy(2, c, chunk).start()

            @pl.when(jnp.logical_not(self.end))
            def _():
                self.copy(0, c, chunk).start()
                self.copy(1, self.near_end, chunk).start()
                self.copy(0, self.other, chunk).start()
                self.copy(2, self.near_end, chunk).start()
                self.copy(2, self.other, chunk).start()

            return carry

        lax.fori_loop(0, N_CHUNK, one, 0)

    def relay(self, chunk):
        @pl.when(jnp.logical_not(self.end))
        def _():
            self.inner.wait(self.inner.r, self.far_end, chunk)
            self.copy(0, self.far_end, chunk).start()
            self.copy(2, self.far_end, chunk).start()

    def collect(self, chunk):
        @pl.when(self.end)
        def _():
            for step in range(3):
                at = jnp.where(self.c == 0, 1 + step, 2 - step)
                self.inner.wait(self.inner.r, at, chunk)
                self.copy(2, at, chunk).start()

    def finish(self):
        def one(step, carry):
            at, chunk = step // 4, step % 4
            self.copy(2, at, chunk).wait_send()

            @pl.when(jnp.logical_not(self.end))
            def _():
                pl.when(at != self.near_end)(lambda: self.copy(0, at, chunk).wait_send())
                pl.when(at == self.near_end)(lambda: self.copy(1, at, chunk).wait_send())

            return carry

        lax.fori_loop(0, 4 * N_CHUNK, one, 0)


def attend_kernel(
    n_col,
    q, k, v, seg_row, seg_col, x, wo, dy, dy_end, dy_mid,
    heads_out, inv_sum, middle_out, dy_out,
    heads_all, middle, dy_full,
    w_out, part, stage, inbox, rs_send, rs_recv, ag_send, ag_recv, h_send, h_recv, local, flushed,
):
    r, c = lax.axis_index("row"), lax.axis_index("col")
    tok, heads = q.shape
    width = x.shape[1]
    rows = tok // N_CHUNK
    me = r * n_col + c
    row_base = r * n_col
    greet(line_peers(r, c, n_col))
    gather = LateGather(dy_full, ag_send, ag_recv, r, c, n_col, width)
    scatter = Scatter(part, stage, inbox, rs_send, rs_recv, c, n_col)
    everything = pl.ds(0, dy_full.shape[2])
    flush = Flush(((heads_all, heads_out), (middle, middle_out), ((dy_full, everything), dy_out)), flushed, rows)

    def block_load(source, block, sem):
        return pltpu.make_async_copy(
            source.reshape(N_CHUNK, rows, width), dy_full.at[:, :, span(block * width, width)], sem
        )

    own = block_load(dy, me, local.at[0])
    own.start()
    early = [
        block_load(dy_end, row_base + gather.near_end, local.at[1]),
        block_load(dy_mid, row_base + gather.other, local.at[2]),
    ]

    @pl.when(jnp.logical_not(gather.end))
    def _():
        for copy in early:
            copy.start()

    load = pltpu.make_async_copy(wo, w_out, local.at[3])
    load.start()
    own.wait()

    @pl.when(jnp.logical_not(gather.end))
    def _():
        for copy in early:
            copy.wait()

    gather.start()

    def heads_copy(chunk):
        piece = heads_all.at[pl.ds(chunk * rows, rows), span(r * heads, heads)]
        return remote(piece, piece, h_send.at[chunk], h_recv.at[chunk], {"row": 1 - r})

    def attend(chunk):
        at = pl.ds(chunk * rows, rows)
        keys = (chunk + 1) * rows
        allowed = allowed_pairs(seg_col[at, :], seg_row[:, 0:keys], chunk, rows, keys)

        def head_step(head, carry):
            total, inverse = carry
            scores = dot_nt(of_head(q[at, :], head), k[0:keys, :]) * HD**-0.5
            weights = jnp.exp(jnp.where(allowed, scores, masked_score))
            inv = 1.0 / jnp.sum(weights, axis=1, keepdims=True)
            probs = (weights * inv).astype(BF16)
            total = total + dot_nn(probs, of_head(v[0:keys, :], head))
            inverse = jnp.where(lanes((rows, 128)) == head, inv, inverse)
            return total, inverse

        total, inverse = lax.fori_loop(
            0, heads // HD, head_step, (jnp.zeros((rows, heads), F32), jnp.zeros((rows, 128), F32))
        )
        heads_all[at, span(r * heads, heads)] = total.astype(BF16)
        inv_sum[at, :] = inverse

    def contract(chunk):
        part[chunk] = dot_nn(heads_all[span(chunk * rows, rows), :], w_out[...])

    for chunk in range(N_CHUNK):
        attend(chunk)
        heads_copy(chunk).start()
        if chunk == 0:
            load.wait()
        if chunk >= 1:
            scatter.near(chunk - 1)
        if chunk >= 2:
            scatter.far(chunk - 2)
            gather.relay(chunk - 2)
        heads_copy(chunk).wait_recv()
        flush.start(chunk, (0,))
        contract(chunk)
        scatter.open(chunk)
    gather.relay(N_CHUNK - 2)
    gather.relay(N_CHUNK - 1)
    scatter.near(N_CHUNK - 1)
    scatter.far(N_CHUNK - 2)
    gather.collect(0)
    scatter.far(N_CHUNK - 1)

    def settle(chunk, carry):
        at = span(chunk * rows, rows)
        scatter.total(chunk, middle, at)
        middle[at, :] += x[at, :].astype(F32)
        pl.when(chunk > 0)(lambda: gather.collect(chunk))
        gather.inner.wait_other(chunk)
        flush.start(chunk, (1, 2))
        return carry

    lax.fori_loop(0, N_CHUNK, settle, 0)
    gather.finish()
    scatter.finish()
    for chunk in range(N_CHUNK):
        heads_copy(chunk).wait_send()
    flush.finish()


def attend(n_col, q, k, v, seg_row, seg_col, x, wo, dy, dy_end, dy_mid):
    tok, heads = q.shape
    width = x.shape[1]
    shape = jax.ShapeDtypeStruct
    outs = [
        shape((tok, 2 * heads), BF16),
        shape((tok, 128), F32),
        shape((tok, width), F32),
        shape((tok, 2 * n_col * width), BF16),
    ]
    scratch = [
        pltpu.VMEM((tok, 2 * heads), BF16),
        pltpu.VMEM((tok, width), F32),
        pltpu.VMEM((N_CHUNK, tok // N_CHUNK, 2 * n_col * width), BF16),
        pltpu.VMEM(wo.shape, BF16),
        *Scatter.scratch(n_col, tok // N_CHUNK, width),
        *gather_sems(n_col),
        pltpu.SemaphoreType.DMA((N_CHUNK,)),
        pltpu.SemaphoreType.DMA((N_CHUNK,)),
        pltpu.SemaphoreType.DMA((4,)),
        pltpu.SemaphoreType.DMA((3, N_CHUNK)),
    ]
    return kernel_call(
        functools.partial(attend_kernel, n_col), "attend", 2, outs, [True, False, True, True],
        [vmem()] * 6 + [anywhere()] * 4, scratch, 8 * tok * tok * heads,
    )(q, k, v, seg_row, seg_col, x, wo, dy, dy_end, dy_mid)


def ffn_kernel(
    n_col, n_sum,
    middle, gain, dy_full, wg, wu, wd, wg_other, wu_other, wd_other,
    h2_out, units_out, gate_out, up_out, middle_grad_out, branch_out, gain_sum, sum_out,
    units, grad_gate, grad_up, grad_middle, grad_branch,
    full, gate_own, up_own, down_own, gate_far, up_far, scale_wide, grad_two,
    part, stage, inbox, rs_send, rs_recv, held, sent, arrived, st_send, st_recv,
    ag_send, ag_recv, x_send, x_recv, local, flushed, *refs,
):
    r, c = lax.axis_index("row"), lax.axis_index("col")
    tok, width = middle.shape
    half = n_col * width
    n_unit = down_own.shape[0]
    rows = tok // N_CHUNK
    me = r * n_col + c
    sums = refs[0:1]

    def chunk_rows(chunk):
        return span(chunk * rows, rows)

    gather = Gather(full, ag_send, ag_recv, r, c, n_col, width)
    scatter = Scatter(part, stage, inbox, rs_send, rs_recv, c, n_col)
    totals = Totals(held, sent, arrived, st_send, st_recv, r, c)
    mine, far = span(r * n_unit, n_unit), span((1 - r) * n_unit, n_unit)
    near_rows, far_rows = span(r * half, half), span((1 - r) * half, half)
    flush = Flush(
        (
            ((full, near_rows), h2_out), (grad_gate, gate_out), (grad_up, up_out), (units, units_out),
            (grad_middle, middle_grad_out), (grad_branch, branch_out),
        ),
        flushed, rows,
    )
    loads = [
        pltpu.make_async_copy(src, dst, local.at[n])
        for n, (src, dst) in enumerate(
            (
                (wg.at[:, mine], gate_own.at[near_rows, :]),
                (wg_other, gate_own.at[far_rows, :]),
                (wu.at[:, mine], up_own.at[near_rows, :]),
                (wu_other, up_own.at[far_rows, :]),
                (wd.at[mine, :], down_own.at[:, near_rows]),
                (wd_other, down_own.at[:, far_rows]),
                (wg.at[:, far], gate_far),
                (wu.at[:, far], up_far),
            )
        )
    ]
    block = span(me * width, width)
    for chunk in range(N_CHUNK):
        values = middle[chunk * rows : (chunk + 1) * rows, :]
        full[chunk, 0:rows, block] = (values * gain[...]).astype(BF16)
        put_notes(full, chunk, block, (as_row(jnp.sum(values * values, axis=1, keepdims=True)),))
    panels = []
    if n_sum:
        tile = tile_of(units, dy_full, sums[0].shape[0], r * half, half // 2)
        panels.append(Reduce(tile, sums, *refs[1:]))
    greet(group_peers(r, c, n_col) + (square_peers() if n_sum else []))
    gather.start(0)
    gather.start(1)
    for copy in loads:
        copy.start()

    def exchange(n, chunk):
        piece = (grad_gate, grad_up, units)[n].at[chunk_rows(chunk), mine]
        return remote(piece, piece, x_send.at[n, chunk], x_recv.at[n, chunk], {"row": 1 - r})

    def norm(chunk):
        square = jnp.zeros((1, rows), F32)
        for at in range(2 * n_col):
            square = square + get_note(full, chunk, pl.ds(at * width, width), 0)
        scale = lax.rsqrt(as_column(square) * (1.0 / (2 * half)) + norm_eps)
        scale_wide[chunk_rows(chunk), :] = jnp.broadcast_to(scale, (rows, scale_wide.shape[1]))

    tile = n_unit // 2

    def units_part(chunk, step):
        at = chunk_rows(chunk)
        scale = scale_wide[at, 0:1]
        cols = span(step * tile, tile)
        gate = dot_nn(full[chunk, 0:rows, :], gate_own[:, cols]) * scale
        up = dot_nn(full[chunk, 0:rows, :], up_own[:, cols]) * scale
        grad = dot_nt(dy_full[at, :], down_own[cols, :])
        sig = jax.nn.sigmoid(gate)
        act = gate * sig
        put = span(r * n_unit + step * tile, tile)
        units[at, put] = (act * up).astype(BF16)
        grad = grad * scale
        grad_gate[at, put] = (grad * up * sig * (1.0 + gate * (1.0 - sig))).astype(BF16)
        grad_up[at, put] = (grad * act).astype(BF16)

    def back(chunk):
        at = chunk_rows(chunk)
        part[chunk] = dot_nt(grad_gate[at, mine], gate_own[near_rows, :]) + dot_nt(
            grad_up[at, mine], up_own[near_rows, :]
        )
        for n in range(3):
            exchange(n, chunk).wait_recv()
        flush.start(chunk, (0, 1, 2, 3))
        part[chunk] += dot_nt(grad_gate[at, far], gate_far[...]) + dot_nt(grad_up[at, far], up_far[...])
        scatter.open(chunk)

    def settle(chunk):
        at = chunk_rows(chunk)
        scatter.total(chunk, grad_two, at)
        product = grad_two[at, :] * middle[at, :]
        totals.note(chunk, jnp.sum(product * gain[...], axis=1, keepdims=True))
        gain_sum[...] += jnp.sum(product.reshape(rows // 8, 8, width), axis=0)

    def conclude(chunk):
        at = chunk_rows(chunk)
        mean = totals.column(chunk) * (1.0 / (2 * half))
        scale = scale_wide[at, 0:1]
        grad = (
            dy_full[at, span(me * width, width)].astype(F32)
            + grad_two[at, :] * gain[...]
            - middle[at, :] * (scale * scale * mean)
        )
        grad_middle[at, :] = grad
        grad_branch[at, :] = grad.astype(BF16)
        flush.start(chunk, (4, 5))

    gain_sum[...] = jnp.zeros_like(gain_sum)
    gather.tick(0)
    gather.start(2)
    gather.tick(1)
    gather.start(3)
    gather.tick(2)
    for copy in loads:
        copy.wait()

    def step(now, carry):
        @pl.when(now < N_CHUNK)
        def _():
            gather.wait_other(now)
            norm(now)

            def part_step(n, carry):
                units_part(now, n)
                return carry

            lax.fori_loop(0, 2, part_step, 0)
            for n in range(3):
                exchange(n, now).start()

        pl.when((now >= 1) & (now <= N_CHUNK))(lambda: scatter.near(now - 1))
        pl.when((now >= 2) & (now <= N_CHUNK + 1))(lambda: scatter.far(now - 2))
        pl.when(now < N_CHUNK)(lambda: back(now))
        gather.tick(now + 3)
        pl.when((now >= 3) & (now <= N_CHUNK + 2))(lambda: settle(now - 3))
        for panel in panels:
            pl.when(now == N_CHUNK - 1)(panel.first)
            pl.when(now == N_CHUNK + 1)(panel.second)
            pl.when(now == N_CHUNK + 1)(panel.merge)
        return carry

    lax.fori_loop(0, N_CHUNK + 3, step, 0)
    totals.exchange()

    def close_up(chunk, carry):
        conclude(chunk)
        return carry

    lax.fori_loop(0, N_CHUNK, close_up, 0)
    gather.finish()
    scatter.finish()
    totals.finish()
    stores = []
    for panel in panels:
        panel.last()
        stores += fetches([(sums[0], sum_out)], local.at[pl.ds(8, 1)])
        panel.finish()

    def close(chunk, carry):
        for n in range(3):
            exchange(n, chunk).wait_send()
        return carry

    lax.fori_loop(0, N_CHUNK, close, 0)
    for copy in stores:
        copy.wait()
    flush.finish()


def ffn(n_col, n_dp, middle, gain, dy_full, wg, wu, wd, wg_other, wu_other, wd_other):
    tok, width = middle.shape
    half, n_unit = n_col * width, wg.shape[1] // 2
    shape = jax.ShapeDtypeStruct
    outs = [
        shape((tok, half), BF16),
        shape((tok, 2 * n_unit), BF16), shape((tok, 2 * n_unit), BF16), shape((tok, 2 * n_unit), BF16),
        shape((tok, width), F32), shape((tok, width), BF16), shape((8, width), F32),
    ]
    n_sum = int(n_dp == 4)
    size = (wd.shape[0] // 4, half // 2) if n_sum else (8, 128)
    outs.append(shape(size, F32))
    rows = tok // N_CHUNK
    scratch = [
        *[pltpu.VMEM((tok, 2 * n_unit), BF16)] * 3,
        pltpu.VMEM((tok, width), F32),
        pltpu.VMEM((tok, width), BF16),
        pltpu.VMEM((N_CHUNK, rows + N_NOTE, 2 * half), BF16),
        pltpu.VMEM((2 * half, n_unit), BF16),
        pltpu.VMEM((2 * half, n_unit), BF16),
        pltpu.VMEM((n_unit, 2 * half), BF16),
        pltpu.VMEM((half, n_unit), BF16),
        pltpu.VMEM((half, n_unit), BF16),
        pltpu.VMEM((tok, 128), F32),
        pltpu.VMEM((tok, width), F32),
        *Scatter.scratch(n_col, rows, width),
        *Totals.scratch(rows),
        *gather_sems(n_col),
        pltpu.SemaphoreType.DMA((3, N_CHUNK)),
        pltpu.SemaphoreType.DMA((3, N_CHUNK)),
        pltpu.SemaphoreType.DMA((9,)),
        pltpu.SemaphoreType.DMA((6, N_CHUNK)),
    ]
    if n_sum:
        scratch += [pltpu.VMEM(size, F32), *Reduce.scratch(size[0], size[1] // 2)]
    return kernel_call(
        functools.partial(ffn_kernel, n_col, n_sum), "ffn", 3, outs, [True] * 6 + [False, True],
        [vmem()] * 3 + [anywhere()] * 6, scratch, 20 * tok * half * n_unit,
    )(middle, gain, dy_full, wg, wu, wd, wg_other, wu_other, wd_other)


class Reduce:
    def __init__(self, tile, outs, stage_one, inbox_one, stage_two, inbox_two, send, recv):
        d = lax.axis_index("dp")
        self.x, self.y = d % 2, d // 2
        self.tile, self.outs = tile, outs
        self.stage_one, self.inbox_one = stage_one, inbox_one
        self.stage_two, self.inbox_two = stage_two, inbox_two
        self.send, self.recv = send, recv
        self.along_x = {"dp": self.y * 2 + 1 - self.x}
        self.along_y = {"dp": (1 - self.y) * 2 + self.x}

    def along(self, side):
        return {"dp": jnp.where(side == 0, self.along_x["dp"], self.along_y["dp"])}

    def copy_one(self, side, n):
        return remote(
            self.stage_one.at[side, n], self.inbox_one.at[side, n],
            self.send.at[side, n], self.recv.at[side, n], self.along(side),
        )

    def copy_two(self, side):
        return remote(
            self.stage_two.at[side], self.inbox_two.at[side],
            self.send.at[side, 2], self.recv.at[side, 2], self.along(1 - side),
        )

    def first(self):
        def one(step, carry):
            side = step % 2
            near = jnp.where(side == 0, self.y, self.x)
            n = jnp.where(step < 2, 1 - near, near)
            owner = jnp.where(side == 0, n * 2 + 1 - self.x, (1 - self.y) * 2 + n)
            self.stage_one[side, n] = self.tile(owner, side).astype(BF16)
            self.copy_one(side, n).start()
            return carry

        lax.fori_loop(0, 4, one, 0)

    def second(self):
        def one(side, carry):
            n = jnp.where(side == 0, 1 - self.y, 1 - self.x)
            owner = jnp.where(side == 0, n * 2 + self.x, self.y * 2 + n)
            value = self.tile(owner, side)
            self.copy_one(side, n).wait_recv()
            self.stage_two[side] = (value + self.inbox_one[side, n].astype(F32)).astype(BF16)
            self.copy_two(side).start()
            return carry

        lax.fori_loop(0, 2, one, 0)

    def put(self, side, value, add):
        each = value.shape[1] // len(self.outs)
        cols = span(side * each, each)
        for n, out in enumerate(self.outs):
            term = value[:, n * each : (n + 1) * each]
            out[:, cols] = out[:, cols] + term if add else term

    def merge(self):
        def one(side, carry):
            n = jnp.where(side == 0, self.y, self.x)
            value = self.tile(self.y * 2 + self.x, side)
            self.copy_one(side, n).wait_recv()
            self.put(side, value + self.inbox_one[side, n].astype(F32), False)
            return carry

        lax.fori_loop(0, 2, one, 0)

    def last(self):
        def one(side, carry):
            self.copy_two(side).wait_recv()
            self.put(side, self.inbox_two[side].astype(F32), True)
            return carry

        lax.fori_loop(0, 2, one, 0)

    def finish(self):
        def one(side, carry):
            for n in range(2):
                self.copy_one(side, n).wait_send()
            self.copy_two(side).wait_send()
            return carry

        lax.fori_loop(0, 2, one, 0)

    @staticmethod
    def scratch(rows, cols):
        return [
            pltpu.VMEM((2, 2, rows, cols), BF16),
            pltpu.VMEM((2, 2, rows, cols), BF16),
            pltpu.VMEM((2, rows, cols), BF16),
            pltpu.VMEM((2, rows, cols), BF16),
            pltpu.SemaphoreType.DMA((2, 3)),
            pltpu.SemaphoreType.DMA((2, 3)),
        ]


def square_peers():
    d = lax.axis_index("dp")
    x, y = d % 2, d // 2
    always = d >= 0
    return [(always, {"dp": y * 2 + 1 - x}), (always, {"dp": (1 - y) * 2 + x})]


def tile_of(left, right, n_row, base=0, width=None):
    cols = (right.shape[1] if width is None else width) // 2

    def tile(owner, side):
        return dot_tn(left[:, span(owner * n_row, n_row)], right[:, span(base + side * cols, cols)])

    return tile


def branch_kernel(
    n_col, n_sum,
    branch, units_in, wd, middle_in, dy_full, h2_in, gate_in, wo, wo_other, heads_in,
    *refs,
):
    (output_out, heads_out, half_out), refs = refs[:3], refs[3:]
    sums_out, refs = refs[:n_sum], refs[n_sum:]
    (
        units, middle, h2, grad_gate, heads_all, branch_half, output, grad_heads,
        full, down, dy_half, w_out, part, stage, inbox, rs_send, rs_recv, ag_send, ag_recv, local, flushed,
    ), refs = refs[:21], refs[21:]
    sums, refs = refs[:n_sum], refs[n_sum:]
    r, c = lax.axis_index("row"), lax.axis_index("col")
    tok, width = middle.shape
    half = n_col * width
    heads = grad_heads.shape[1]
    rows = tok // N_CHUNK
    me = r * n_col + c
    mine, other = span(r * half, half), span((1 - r) * half, half)
    own, dy_load, units_load, down_load, *loads = fetches(
        [
            (branch.reshape(N_CHUNK, rows, width), full.at[:, :, span(me * width, width)]),
            (dy_full.at[:, mine], dy_half),
            (units_in, units),
            (wd, down),
            (h2_in, h2),
            (gate_in, grad_gate),
            (wo.at[span(r * heads, heads), :], w_out.at[:, mine]),
            (wo_other, w_out.at[:, other]),
            (middle_in, middle),
            (heads_in, heads_all),
        ],
        local,
    )
    greet(line_peers(r, c, n_col) + (square_peers() if n_sum else []))
    gather = Gather(full, ag_send, ag_recv, r, c, n_col, width)
    scatter = Scatter(part, stage, inbox, rs_send, rs_recv, c, n_col)
    flush = Flush(((output, output_out), (grad_heads, heads_out), (branch_half, half_out)), flushed, rows)
    own.wait()

    def begin_gather(chunk, carry):
        gather.start(chunk)
        return carry

    lax.fori_loop(0, N_CHUNK, begin_gather, 0)
    panels = []
    if n_sum:
        terms = ((units, dy_half, half // 2, half // 2), (h2, grad_gate, 0, None), (heads_all, branch_half, 0, None))
        for n, (left, right, base, cols) in enumerate(terms):
            tile = tile_of(left, right, sums[n].shape[0], base, cols)
            panels.append(Reduce(tile, (sums[n],), *refs[6 * n : 6 * n + 6]))
    dy_load.wait()
    units_load.wait()
    for panel in panels[:1]:
        panel.first()
    down_load.wait()

    def begin(chunk, carry):
        part[chunk] = dot_nn(units[span(chunk * rows, rows), :], down[...])
        scatter.open(chunk)
        gather.relay(1, chunk)
        return carry

    lax.fori_loop(0, N_CHUNK, begin, 0)
    for copy in loads:
        copy.wait()
    for panel in panels[1:2]:
        panel.first()

    def carry_on(chunk, carry):
        gather.relay(2, chunk)
        scatter.near(chunk)
        return carry

    lax.fori_loop(0, N_CHUNK, carry_on, 0)
    for panel in panels[:1]:
        panel.second()

    def arrive(chunk, carry):
        gather.relay(3, chunk)
        scatter.far(chunk)
        return carry

    lax.fori_loop(0, N_CHUNK, arrive, 0)

    def copy_half(chunk, carry):
        gather.wait_other(chunk)
        branch_half[span(chunk * rows, rows), :] = full[chunk, :, mine]
        return carry

    lax.fori_loop(0, N_CHUNK, copy_half, 0)
    for panel in panels[2:]:
        panel.first()
    for panel in panels[:1]:
        panel.merge()
    for panel in panels[1:2]:
        panel.second()

    def settle(chunk, carry):
        at = span(chunk * rows, rows)
        grad_heads[at, :] = dot_nt(full[chunk], w_out[...]).astype(BF16)
        scatter.total(chunk, output, at)
        output[at, :] += middle[at, :]
        flush.start(chunk)
        return carry

    lax.fori_loop(0, N_CHUNK, settle, 0)
    for panel in panels[1:2]:
        panel.merge()
    for panel in panels[2:]:
        panel.second()
        panel.merge()
    stores = []
    for n, panel in enumerate(panels):
        panel.last()
        stores += fetches([(sums[n], sums_out[n])], local.at[pl.ds(10 + n, 1)])
    gather.finish()
    scatter.finish()
    for panel in panels:
        panel.finish()
    for copy in stores:
        copy.wait()
    flush.finish()


def branch_back(n_col, n_dp, branch, units, wd, middle, dy_full, h2, grad_gate, wo, wo_other, heads_all):
    tok, width = middle.shape
    half, heads = n_col * width, wo_other.shape[0]
    rows = tok // N_CHUNK
    shape = jax.ShapeDtypeStruct
    outs = [shape((tok, width), F32), shape((tok, heads), BF16), shape((tok, half), BF16)]
    scratch = [
        pltpu.VMEM(units.shape, BF16),
        pltpu.VMEM(middle.shape, F32),
        pltpu.VMEM(h2.shape, BF16),
        pltpu.VMEM(grad_gate.shape, BF16),
        pltpu.VMEM(heads_all.shape, BF16),
        pltpu.VMEM((tok, half), BF16),
        pltpu.VMEM((tok, width), F32),
        pltpu.VMEM((tok, heads), BF16),
        pltpu.VMEM((N_CHUNK, rows, 2 * half), BF16),
        pltpu.VMEM(wd.shape, BF16),
        pltpu.VMEM((tok, half), BF16),
        pltpu.VMEM((heads, 2 * half), BF16),
        *Scatter.scratch(n_col, rows, width),
        *gather_sems(n_col),
        pltpu.SemaphoreType.DMA((13,)),
        pltpu.SemaphoreType.DMA((3, N_CHUNK)),
    ]
    n_sum = 0
    if n_dp == 4:
        n_sum = 3
        sizes = [(wd.shape[0] // 4, half // 2), (half // 4, grad_gate.shape[1]), (heads // 2, half)]
        outs += [shape(size, F32) for size in sizes]
        scratch += [pltpu.VMEM(size, F32) for size in sizes]
        for size in sizes:
            scratch += Reduce.scratch(size[0], size[1] // 2)
    return kernel_call(
        functools.partial(branch_kernel, n_col, n_sum), "branch", 4, outs, [True] * len(outs),
        [anywhere()] * 10, scratch, 12 * tok * half * half,
    )(branch, units, wd, middle, dy_full, h2, grad_gate, wo, wo_other, heads_all)


def attend_back_kernel(
    n_col, n_dp, n_sum,
    q_in, k_in, v_in, heads_grad_in, seg_row, seg_col_in, inv_in, cos_in, sin_in, x_in, r1_in, gain, middle_in,
    gain_two, h1_in, wq, wk, wv, h2_in, up_in,
    *refs,
):
    (tokens_out, gain_sums, triple_out), refs = refs[:3], refs[3:]
    sums_out, refs = refs[:n_sum], refs[n_sum:]
    (
        q, k, v, grad_heads, seg_col, inv_sum, cos_table, sin_table, x, r1, grad_middle,
        h1, h2, grad_up, grad_tokens, triple,
        weights, grad_k, grad_v, grad_q, grad_one, gain_mine, gain_box, part, stage, inbox, rs_send, rs_recv,
        held, sent, arrived, st_send, st_recv, x_send, x_recv, g_send, g_recv, local, flushed,
    ), refs = refs[:39], refs[39:]
    sums, refs = refs[:n_sum], refs[n_sum:]
    r, c, d = lax.axis_index("row"), lax.axis_index("col"), lax.axis_index("dp")
    tok, width = x.shape
    half = n_col * width
    heads = q.shape[1]
    rows = tok // N_CHUNK
    me = r * n_col + c
    early = [(h2_in, h2), (up_in, grad_up)]
    first = [
        (q_in, q), (k_in, k), (v_in, v), (heads_grad_in, grad_heads), (seg_col_in, seg_col), (inv_in, inv_sum),
        (cos_in, cos_table), (sin_in, sin_table),
    ]
    later = [(h1_in, h1), (x_in, x), (r1_in, r1)]
    later.append((middle_in, grad_middle))
    for n, w in enumerate((wq, wk, wv)):
        for side in range(2):
            later.append(
                (w.at[:, pl.ds(side * heads, heads)], weights.at[:, pl.ds((side * 3 + n) * heads, heads)])
            )
    copies = fetches(early + first + later, local)
    early, first, later = copies[:2], copies[2:10], copies[10:]
    dp_peers = [(d != at, {"dp": jnp.int32(at)}) for at in range(n_dp)]
    greet(group_peers(r, c, n_col) + dp_peers)
    scatter = Scatter(part, stage, inbox, rs_send, rs_recv, c, n_col)
    totals = Totals(held, sent, arrived, st_send, st_recv, r, c)
    flush = Flush(((grad_tokens, tokens_out),), flushed, rows)
    panels = []
    if n_sum:
        for n, (left, right) in enumerate(((h2, grad_up), (h1, triple))):
            tile = tile_of(left, right, sums[n].shape[0])
            panels.append(Reduce(tile, sums[1:] if n else sums[:1], *refs[6 * n : 6 * n + 6]))

    def exchange(chunk):
        piece = triple.at[span(chunk * rows, rows), span(r * 3 * heads, 3 * heads)]
        return remote(piece, piece, x_send.at[chunk], x_recv.at[chunk], {"row": 1 - r})

    def attend(chunk):
        at = pl.ds(chunk * rows, rows)
        keys = (chunk + 1) * rows
        allowed = allowed_pairs(seg_col[at, :], seg_row[:, 0:keys], chunk, rows, keys)
        grad_q[...] = jnp.zeros_like(grad_q)

        def head_step(head, carry):
            query = of_head(q[at, :], head)
            grad = of_head(grad_heads[at, :], head)
            scores = dot_nt(query, k[0:keys, :]) * HD**-0.5
            inv = jnp.sum(jnp.where(lanes((rows, 128)) == head, inv_sum[at, :], 0.0), axis=1, keepdims=True)
            probs = jnp.exp(jnp.where(allowed, scores, masked_score)) * inv
            grad_probs = dot_nt(grad, v[0:keys, :])
            weighted = jnp.sum(probs * grad_probs, axis=1, keepdims=True)
            grad_scores = (probs * (grad_probs - weighted) * HD**-0.5).astype(BF16)
            grad_q[...] += dot_nn(grad_scores, of_head(k[0:keys, :], head))
            grad_k[0:keys, :] += dot_tn(grad_scores, query)
            grad_v[0:keys, :] += dot_tn(probs.astype(BF16), grad)
            return carry

        lax.fori_loop(0, heads // HD, head_step, 0)
        cos_rows = widen(cos_table[at, :], heads)
        sin_rows = widen(sin_table[at, :], heads)
        for n, value in enumerate((grad_q[...], grad_k[at, :])):
            value = value * cos_rows - swap_halves(value) * sin_rows
            triple[at, span((r * 3 + n) * heads, heads)] = value.astype(BF16)
        triple[at, span((r * 3 + 2) * heads, heads)] = grad_v[at, :].astype(BF16)
        exchange(chunk).start()

    def contract(chunk):
        at = span(chunk * rows, rows)
        exchange(chunk).wait_recv()
        part[chunk] = dot_nt(triple[at, :], weights[...])
        scatter.open(chunk)

    def settle(chunk):
        at = span(chunk * rows, rows)
        scatter.total(chunk, grad_one, at)
        product = grad_one[at, :] * (x[at, :].astype(F32) * r1[at, 0:1])
        totals.note(chunk, jnp.sum(product * gain[...], axis=1, keepdims=True))
        gain_mine[0] += jnp.sum(product.reshape(rows // 8, 8, width), axis=0)

    def conclude(chunk):
        at = span(chunk * rows, rows)
        mean = totals.column(chunk) * (1.0 / (2 * half))
        scale = r1[at, 0:1]
        grad_tokens[at, :] = grad_middle[at, :] + scale * (
            grad_one[at, :] * gain[...] - x[at, :].astype(F32) * (scale * mean)
        )
        flush.start(chunk)

    def gain_copy(at):
        return remote(gain_box.at[d], gain_box.at[d], g_send.at[at], g_recv.at[d], {"dp": at})

    def gain_arrival(at):
        return remote(gain_box.at[at], gain_box.at[at], g_send.at[at], g_recv.at[at], {"dp": at})

    def others(act):
        def one(at, carry):
            pl.when(at != d)(lambda: act(at))
            return carry

        lax.fori_loop(0, n_dp, one, 0)

    def panel_do(n, what):
        if n_sum:
            getattr(panels[n], what)()

    gain_mine[0] = jnp.zeros(gain_mine.shape[1:], F32)
    gain_mine[1] = gain_two[...]
    grad_k[...] = jnp.zeros_like(grad_k)
    grad_v[...] = jnp.zeros_like(grad_v)
    last = N_CHUNK - 1
    for copy in early:
        copy.wait()
    panel_do(0, "first")
    for copy in first:
        copy.wait()
    attend(last)
    for copy in later:
        copy.wait()
    attend(last - 1)
    contract(last)
    panel_do(0, "second")
    attend(last - 2)
    contract(last - 1)
    scatter.near(last)
    attend(last - 3)
    contract(last - 2)
    scatter.near(last - 1)
    scatter.far(last)
    contract(last - 3)
    panel_do(1, "first")
    scatter.near(last - 2)
    scatter.far(last - 1)
    panel_do(0, "merge")
    settle(last)
    scatter.near(last - 3)
    scatter.far(last - 2)
    panel_do(1, "second")

    def settle_step(now, carry):
        pl.when(now == 1)(lambda: scatter.far(0))
        settle(last - now)
        return carry

    lax.fori_loop(1, N_CHUNK, settle_step, 0)
    gain_box[d] = gain_mine[...]
    others(lambda at: gain_copy(at).start())
    panel_do(1, "merge")
    totals.exchange()

    def close_up(step, carry):
        conclude(last - step)
        return carry

    lax.fori_loop(0, N_CHUNK, close_up, 0)
    others(lambda at: gain_arrival(at).wait_recv())
    gain_total = gain_box[0]
    for at in range(1, n_dp):
        gain_total = gain_total + gain_box[at]
    gain_sums[...] = gain_total
    stores = []
    where = len(copies)
    for n, panel in enumerate(panels):
        panel.last()
        for m in range(1, n_sum) if n else range(1):
            stores += fetches([(sums[m], sums_out[m])], local.at[pl.ds(where + m, 1)])
    if not n_sum:
        stores += fetches([(triple, triple_out)], local.at[pl.ds(where, 1)])
    scatter.finish()
    totals.finish()
    for chunk in range(N_CHUNK):
        exchange(chunk).wait_send()
    others(lambda at: gain_copy(at).wait_send())
    for panel in panels:
        panel.finish()
    for copy in stores:
        copy.wait()
    flush.finish()


def attend_back(
    n_col, n_dp,
    q, k, v, grad_heads, seg_row, seg_col, inv_sum, cos_table, sin_table, x, r1, gain, grad_middle,
    gain_two, h1, wq, wk, wv, h2, grad_up,
):
    tok, width = x.shape
    half, heads = n_col * width, q.shape[1]
    rows = tok // N_CHUNK
    shape = jax.ShapeDtypeStruct
    triple = (tok, 6 * heads) if n_dp != 4 else (8, 128)
    outs = [shape((tok, width), F32), shape((2, 8, width), F32), shape(triple, BF16)]
    held = [q, k, v, grad_heads, seg_col, inv_sum, cos_table, sin_table, x, r1, grad_middle]
    held += [h1, h2, grad_up]
    scratch = [
        *[pltpu.VMEM(array.shape, array.dtype) for array in held],
        pltpu.VMEM((tok, width), F32),
        pltpu.VMEM((tok, 6 * heads), BF16),
        pltpu.VMEM((half, 6 * heads), BF16),
        pltpu.VMEM((tok, heads), F32),
        pltpu.VMEM((tok, heads), F32),
        pltpu.VMEM((rows, heads), F32),
        pltpu.VMEM((tok, width), F32),
        pltpu.VMEM((2, 8, width), F32),
        pltpu.VMEM((n_dp, 2, 8, width), F32),
        *Scatter.scratch(n_col, rows, width),
        *Totals.scratch(rows),
        pltpu.SemaphoreType.DMA((N_CHUNK,)),
        pltpu.SemaphoreType.DMA((N_CHUNK,)),
        pltpu.SemaphoreType.DMA((n_dp,)),
        pltpu.SemaphoreType.DMA((n_dp,)),
        pltpu.SemaphoreType.DMA((27,)),
        pltpu.SemaphoreType.DMA((1, N_CHUNK)),
    ]
    n_sum = 0
    if n_dp == 4:
        sizes = [(half // 4, grad_up.shape[1])] + [(half // 4, 2 * heads)] * 3
        n_sum = len(sizes)
        outs += [shape(size, F32) for size in sizes]
        scratch += [pltpu.VMEM(size, F32) for size in sizes]
        for size in sizes[:1] + [(half // 4, 6 * heads)]:
            scratch += Reduce.scratch(size[0], size[1] // 2)
    return kernel_call(
        functools.partial(attend_back_kernel, n_col, n_dp, n_sum), "attend_back", 5, outs,
        [True, False, True] + [True] * n_sum,
        [anywhere()] * 4 + [vmem()] + [anywhere()] * 6 + [vmem(), anywhere(), vmem()] + [anywhere()] * 6,
        scratch, 16 * tok * tok * heads,
    )(
        q, k, v, grad_heads, seg_row, seg_col, inv_sum, cos_table, sin_table, x, r1, gain, grad_middle,
        gain_two, h1, wq, wk, wv, h2, grad_up,
    )


def finish_kernel(groups, share, gain_sums, *refs):
    n_copy = sum(groups)
    sources, refs = refs[:n_copy], refs[n_copy:]
    gain_out, refs = refs[:2], refs[2:]
    results, refs = refs[: len(groups)], refs[len(groups) :]
    held, (get, put) = refs[:n_copy], refs[n_copy:]
    targets = []
    for result, parts in zip(results, groups):
        cols = result.shape[1] // parts
        targets += [result.at[:, pl.ds(part * cols, cols)] for part in range(parts)]
    pieces = 2
    inward, outward = [], []
    for n, (source, keep, target) in enumerate(zip(sources, held, targets)):
        rows = keep.shape[0] // pieces
        for piece in range(pieces):
            at = pl.ds(piece * rows, rows)
            inward.append(pltpu.make_async_copy(source.at[at, :], keep.at[at, :], get.at[n, piece]))
            outward.append(pltpu.make_async_copy(keep.at[at, :], target.at[at, :], put.at[n, piece]))
    for copy in inward:
        copy.start()
    d = lax.axis_index("dp")
    width = gain_sums.shape[-1]
    shift = lax.rem(width - d * share, width)
    for n in range(2):
        moved = pltpu.roll(gain_sums[n], shift, 1)
        gain_out[n][...] = jnp.sum(moved, axis=0, keepdims=True)[:, 0:share]
    for one, two in zip(inward, outward):
        one.wait()
        two.start()
    for copy in outward:
        copy.wait()


def finish(share, gain_sums, arrays):
    shape = jax.ShapeDtypeStruct
    groups = tuple(len(parts) for parts in arrays)
    flat = [part for parts in arrays for part in parts]
    outs = [shape((1, share), F32)] * 2
    outs += [shape((p[0].shape[0], sum(x.shape[1] for x in p)), p[0].dtype) for p in arrays]
    n_copy = len(flat)
    return pl.pallas_call(
        functools.partial(finish_kernel, groups, share),
        out_shape=outs,
        in_specs=[vmem()] + [anywhere()] * n_copy,
        out_specs=[vmem()] * 2 + [anywhere()] * len(arrays),
        scratch_shapes=[pltpu.VMEM(x.shape, x.dtype) for x in flat]
        + [pltpu.SemaphoreType.DMA((n_copy, 2)), pltpu.SemaphoreType.DMA((n_copy, 2))],
        compiler_params=pltpu.CompilerParams(vmem_limit_bytes=VMEM_LIMIT),
        name="finish",
    )(gain_sums, *flat)


def body(
    n_dp,
    n_col,
    tokens,
    gain_attn,
    gain_ffn,
    w_query,
    w_key,
    w_value,
    w_out,
    w_gate,
    w_up,
    w_down,
    grad_output,
    segments,
    positions,
):
    tok, width = tokens.shape
    heads = w_query.shape[1] // 2
    gain_one, gain_two = gain_attn.reshape(1, width), gain_ffn.reshape(1, width)
    (
        q, k, v, h1, r1, cos_table, sin_table, seg_col, dy_end, dy_mid, wo_other, wg_other, wu_other, wd_other,
    ) = project(
        n_col, tokens, gain_one, positions, segments, grad_output,
        w_query, w_key, w_value, w_out, w_gate, w_up, w_down,
    )
    heads_all, inv_sum, middle, dy_full = attend(
        n_col, q, k, v, segments, seg_col, tokens, w_out, grad_output, dy_end, dy_mid
    )
    h2, units, grad_gate, grad_up, grad_middle, branch, gain_sum, down_one = ffn(
        n_col, n_dp, middle, gain_two, dy_full, w_gate, w_up, w_down, wg_other, wu_other, wd_other
    )
    output, grad_heads, branch_half, *sums_one = branch_back(
        n_col, n_dp, branch, units, w_down, middle, dy_full, h2, grad_gate, w_out, wo_other, heads_all
    )
    grad_tokens, gain_sums, triple, *sums_two = attend_back(
        n_col, n_dp, q, k, v, grad_heads, segments, seg_col, inv_sum, cos_table, sin_table, tokens, r1,
        gain_one, grad_middle, gain_sum, h1, w_query, w_key, w_value, h2, grad_up,
    )
    if n_dp == 4:
        down_two, grad_wg, grad_wo = sums_one
        grad_wd = (down_one, down_two)
        grad_wu, *grad_qkv = sums_two
    else:

        def summed(left, right):
            grad = jnp.einsum("ta,tb->ab", left, right, preferred_element_type=F32).astype(BF16)
            return lax.psum_scatter(grad, "dp", scatter_dimension=0, tiled=True).astype(F32)

        row = lax.axis_index("row")
        dy_half = lax.dynamic_slice(dy_full, (0, row * n_col * width), (tok, n_col * width))
        grad_wd, grad_wg = (summed(units, dy_half),), summed(h2, grad_gate)
        grad_wu, grad_wo = summed(h2, grad_up), summed(heads_all, branch_half)
        parts = summed(h1, triple).reshape(-1, 2, 3, heads)
        grad_qkv = [parts[:, :, n].reshape(-1, 2 * heads) for n in range(3)]
    gain_a, gain_b, *results = finish(
        width // n_dp, gain_sums,
        [(m,) for m in (output, grad_tokens, *grad_qkv, grad_wo, grad_wg, grad_wu)] + [grad_wd],
    )
    blocks = [m.reshape((1, 1) + m.shape) for m in results[2:]]
    return (*results[:2], gain_a.reshape(1, 1, -1), gain_b.reshape(1, 1, -1), *blocks)


def solution(mesh):
    return jax.shard_map(
        functools.partial(body, mesh.shape["dp"], mesh.shape["col"]),
        mesh=mesh,
        in_specs=(
            P("dp", ("row", "col")),
            P(("row", "col")),
            P(("row", "col")),
            P("row", "col"),
            P("row", "col"),
            P("row", "col"),
            P("col", "row"),
            P("row", "col"),
            P("row", "col"),
            P("col", "row"),
            P("dp", ("row", "col")),
            P("dp", None),
            P("dp", None),
        ),
        out_specs=(
            P("dp", ("row", "col")),
            P("dp", ("row", "col")),
            P(("row", "col"), "dp", None),
            P(("row", "col"), "dp", None),
            P("row", "dp", None, "col"),
            P("row", "dp", None, "col"),
            P("row", "dp", None, "col"),
            P("col", "dp", None, "row"),
            P("row", "dp", None, "col"),
            P("row", "dp", None, "col"),
            P("col", "dp", None, "row"),
        ),
        check_vma=False,
    )
```

profile of v0, /device:TPU:0, one launch (start us, length us, event | category | flops | bytes accessed | tf_op | source)
XLA Modules:
  0.0 350.4 jit_solution(13358314884045924934)
XLA Ops:
  0.7 0.6 pad_maximum_fusion.rope
  1.2 49.2 %project.1 = (bf16[1024,256]{1,0:T(8,128)(2,1)}, bf16[1024,256]{1,0:T(8,128)(2,1)}, bf16[1024,256]{1,0:T(8,128)(2,1)}, bf16[1024,1024]{1,0:T(8,128)(2,1)}, f32[1...) custom-call(bf16[1024,256]{1,0:T(8,128)(2,1)} %x_in.1, ...), custom_call_target="tpu_custom_call" | custom-call | flops 3221225472 | bytes 16777216 | tf_op jit(solution)/shard_map/project/pallas_call | solution.py:579
  50.4 56.2 %attend.1 = (bf16[1024,512]{1,0:T(8,128)(2,1)}, f32[1024,128]{1,0:T(8,128)}, f32[1024,256]{1,0:T(8,128)}, bf16[1024,2048]{1,0:T(8,128)(2,1)}) custom-call(bf16[1024,256]{1,0:T(8,128)(2,1)} %get-tuple-element.59.q.q_in, bf16[1024,256]{1,0:T(8,128)(2,1)} %get-tuple-element.60.k.k_in, bf16[1024,256]{1,0:T(8,128)(2,1)} %get-tuple-element.61.v.v_in, ...), custom_call_target="tpu_custom_call" | custom-call | flops 2147483648 | bytes 16777216 | tf_op jit(solution)/shard_map/attend/pallas_call | solution.py:797
  106.6 89.6 %ffn.1 = (bf16[1024,1024]{1,0:T(8,128)(2,1)}, bf16[1024,2048]{1,0:T(8,128)(2,1)}, bf16[1024,2048]{1,0:T(8,128)(2,1)}, bf16[1024,2048]{1,0:T(8,128)(2,1)}, f32[10...) custom-call(f32[1024,256]{1,0:T(8,128)} %get-tuple-element.65.middle.middle_in, ...), custom_call_target="tpu_custom_call" | custom-call | flops 21474836480 | bytes 16777216 | tf_op jit(solution)/shard_map/ffn/pallas_call | solution.py:1021
  196.2 68.0 %branch.1 = (f32[1024,256]{1,0:T(8,128)}, bf16[1024,256]{1,0:T(8,128)(2,1)}, bf16[1024,1024]{1,0:T(8,128)(2,1)}, f32[512,512]{1,0:T(8,128)}, f32[256,2048]{1,0:T(8,128)}, /*index=5*/f32[128,1024]{1,0:T(8,128)}) custom-call(bf16[1024,256]{1,0:T(8,128)(2,1)} %get-tuple-element.70.branch, bf16[1024,2048]{1,0:T(8,128)(2,1)} %get-tuple-element.71.units_in, ...), custom_call_target="tpu_custom_call" | custom-call | flops 12884901888 | bytes 16777216 | tf_op jit(solution)/shard_map/branch/pallas_call | solution.py:1296
  264.2 76.4 %attend_back.1 = (f32[1024,256]{1,0:T(8,128)}, f32[2,8,256]{2,1,0:T(8,128)}, bf16[8,128]{1,0:T(8,128)(2,1)}, f32[256,2048]{1,0:T(8,128)}, f32[256,512]{1,0:T(8,1...) custom-call(bf16[1024,256]{1,0:T(8,128)(2,1)} %get-tuple-element.59.q.q_in, bf16[1024,256]{1,0:T(8,128)(2,1)} %get-tuple-element.60.k.k_in, ...), custom_call_target="tpu_custom_call" | custom-call | flops 4294967296 | bytes 16777216 | tf_op jit(solution)/shard_map/attend_back/pallas_call | solution.py:1535
  340.6 9.6 %finish.1 = (f32[1,64]{1,0:T(1,128)}, f32[1,64]{1,0:T(1,128)}, f32[1024,256]{1,0:T(8,128)}, f32[1024,256]{1,0:T(8,128)}, f32[256,512]{1,0:T(8,128)}, /*index=5*/...) custom-call(f32[2,8,256]{2,1,0:T(8,128)} %get-tuple-element.85.gain_, ...), custom_call_target="tpu_custom_call" | custom-call | tf_op jit(solution)/shard_map/finish/pallas_call | solution.py:1586
  (1 shorter events, 0.0 us)
where the time goes:
time: 351 us; the launch traced here: 350 us
  Pallas kernels  349 us (99%)
    pallas_call x1, Pallas kernels, ffn(): kernel_call(functools.partial(ffn_kernel, n_col, n_sum), 'ffn', 3, outs,...  89.6 us
    pallas_call x1, Pallas kernels, attend_back(): kernel_call(functools.partial(attend_back_kernel, n_col, n_dp, n_sum), 'a...  76.4 us
    pallas_call x1, Pallas kernels, branch_back(): kernel_call(functools.partial(branch_kernel, n_col, n_sum), 'branch', 4,...  68 us
    pallas_call x1, Pallas kernels, attend(): kernel_call(functools.partial(attend_kernel, n_col), 'attend', 2, outs, [...  56.2 us
    pallas_call x1, Pallas kernels, project(): kernel_call(functools.partial(project_kernel, n_col), 'project', 1, outs,...  49.2 us
    pallas_call x1, Pallas kernels, finish(): pl.pallas_call(functools.partial(finish_kernel, groups, share), out_shape...  9.55 us

commit v1 on v0

--- a/solution.py
+++ b/solution.py
@@ -140,6 +140,26 @@
 
             self.copy(2, at, chunk).start()
 
+    def toward(self, way, at, chunk):
+        piece = self.piece(self.r, at, chunk)
+        where = {"col": jnp.clip(self.c - 1 + 2 * way, 0, self.n_col - 1)}
+        return remote(piece, piece, self.send.at[way, at, chunk], self.recv.at[self.r, at, chunk], where)
+
+    def hand(self, at, chunk, way=None):
+        self.wait(self.r, at, chunk)
+        if way is not None:
+            self.toward(way, at, chunk).start()
+        self.copy(2, at, chunk).start()
+
+    def end_relay(self, distance, chunk):
+        self.hand(jnp.where(self.c == 0, distance, 3 - distance), chunk)
+
+    def middle_relay(self, kind, chunk):
+        outward = (self.c == 2).astype(jnp.int32)
+        near_end = 3 * outward
+        at = {"a": 3 - self.c, "b": near_end, "c": 3 - near_end}[kind]
+        self.hand(at, chunk, 1 - outward if kind == "b" else outward)
+
     def tick(self, now):
         for distance in range(self.n_col - 1, 0, -1):
             chunk = now + 1 - distance
@@ -186,15 +206,29 @@
     def term(self, chunk, dest):
         return self.part[chunk, :, span(dest * self.width, self.width)]
 
+    def staged(self, dest):
+        return dest - (dest > self.c).astype(jnp.int32)
+
+    def slot(self, way, dest, at):
+        inner = ((at == 1) & (way == 1)) | ((at == 2) & (way == 0))
+        return jnp.where((dest == at) & inner, 4, dest)
+
     def copy(self, way, chunk, dest):
         where = jnp.clip(self.c + 1 - 2 * way, 0, self.n_col - 1)
+        slot = self.slot(way, dest, where)
         return remote(
-            self.stage.at[chunk, dest],
-            self.inbox.at[way, chunk, dest],
+            self.stage.at[chunk, self.staged(dest)],
+            self.inbox.at[chunk, slot],
             self.send.at[chunk, dest],
-            self.recv.at[way, chunk, dest],
+            self.recv.at[chunk, slot],
             {"col": where},
         )
+
+    def arrival(self, way, chunk, dest):
+        slot = self.slot(way, dest, self.c)
+        here = self.inbox.at[chunk, slot]
+        remote(here, here, self.send.at[chunk, dest], self.recv.at[chunk, slot], {"col": self.c}).wait_recv()
+        return self.inbox[chunk, slot].astype(F32)
 
     def open(self, chunk):
         @pl.when(jnp.logical_not(self.middle))
@@ -203,18 +237,16 @@
 
             def ship(step, carry):
                 dest = jnp.where(way == 0, self.n_col - 1 - step, step)
-                self.stage[chunk, dest] = self.term(chunk, dest).astype(BF16)
+                self.stage[chunk, self.staged(dest)] = self.term(chunk, dest).astype(BF16)
                 self.copy(way, chunk, dest).start()
                 return carry
 
             lax.fori_loop(0, self.n_col - 1, ship, 0)
 
     def pass_on(self, way, chunk, dest):
-        copy = self.copy(way, chunk, dest)
-        copy.wait_recv()
-        total = self.term(chunk, dest) + self.inbox[way, chunk, dest].astype(F32)
-        self.stage[chunk, dest] = total.astype(BF16)
-        copy.start()
+        total = self.term(chunk, dest) + self.arrival(way, chunk, dest)
+        self.stage[chunk, self.staged(dest)] = total.astype(BF16)
+        self.copy(way, chunk, dest).start()
 
     def near(self, chunk):
         @pl.when(self.middle)
@@ -236,13 +268,11 @@
     def total(self, chunk, out, at):
         c = self.c
         way = (c == 0).astype(jnp.int32)
-        self.copy(way, chunk, c).wait_recv()
-        out[at, :] = self.term(chunk, c) + self.inbox[way, chunk, c].astype(F32)
+        out[at, :] = self.term(chunk, c) + self.arrival(way, chunk, c)
 
         @pl.when(self.middle)
         def _():
-            self.copy(1, chunk, c).wait_recv()
-            out[at, :] += self.inbox[1, chunk, c].astype(F32)
+            out[at, :] += self.arrival(1, chunk, c)
 
     def finish(self):
         def one(step, carry):
@@ -260,10 +290,10 @@
     def scratch(n_col, rows, width, n_chunk=N_CHUNK):
         return [
             pltpu.VMEM((n_chunk, rows, n_col * width), F32),
-            pltpu.VMEM((n_chunk, n_col, rows, width), BF16),
-            pltpu.VMEM((2, n_chunk, n_col, rows, width), BF16),
+            pltpu.VMEM((n_chunk, n_col - 1, rows, width), BF16),
+            pltpu.VMEM((n_chunk, n_col + 1, rows, width), BF16),
             pltpu.SemaphoreType.DMA((n_chunk, n_col)),
-            pltpu.SemaphoreType.DMA((2, n_chunk, n_col)),
+            pltpu.SemaphoreType.DMA((n_chunk, n_col + 1)),
         ]
 
 
@@ -611,23 +641,17 @@
             piece, piece, self.inner.send.at[way, at, chunk], self.inner.recv.at[self.inner.r, at, chunk], where
         )
 
-    def start(self):
+    def start(self, chunk):
         c = self.c
-
-        def one(chunk, carry):
-            self.copy(2, c, chunk).start()
-
-            @pl.when(jnp.logical_not(self.end))
-            def _():
-                self.copy(0, c, chunk).start()
-                self.copy(1, self.near_end, chunk).start()
-                self.copy(0, self.other, chunk).start()
-                self.copy(2, self.near_end, chunk).start()
-                self.copy(2, self.other, chunk).start()
-
-            return carry
-
-        lax.fori_loop(0, N_CHUNK, one, 0)
+        self.copy(2, c, chunk).start()
+
+        @pl.when(jnp.logical_not(self.end))
+        def _():
+            self.copy(0, c, chunk).start()
+            self.copy(1, self.near_end, chunk).start()
+            self.copy(0, self.other, chunk).start()
+            self.copy(2, self.near_end, chunk).start()
+            self.copy(2, self.other, chunk).start()
 
     def relay(self, chunk):
         @pl.when(jnp.logical_not(self.end))
@@ -659,52 +683,99 @@
         lax.fori_loop(0, 4 * N_CHUNK, one, 0)
 
 
-def attend_kernel(
-    n_col,
-    q, k, v, seg_row, seg_col, x, wo, dy, dy_end, dy_mid,
+def layer_kernel(
+    n_col, n_sum,
+    q_in, k_in, v_in, seg_row, seg_col_in, x_in, gain, wo, dy, dy_end, dy_mid,
+    wg, wu, wd, wg_other, wu_other, wd_other,
     heads_out, inv_sum, middle_out, dy_out,
-    heads_all, middle, dy_full,
-    w_out, part, stage, inbox, rs_send, rs_recv, ag_send, ag_recv, h_send, h_recv, local, flushed,
+    h2_out, units_out, gate_out, up_out, middle_grad_out, branch_out, gain_sum, sum_out,
+    q, k, v, seg_col, x, heads_all, middle, dy_full, w_out,
+    units, grad_gate, grad_up, grad_middle,
+    full, gate_own, up_own, down_own, gate_far, up_far,
+    part, stage_z, inbox_z, z_send, z_recv, stage_f, inbox_f, f_send, f_recv,
+    held, sent, arrived, t_send, t_recv, dy_send, dy_recv, ag_send, ag_recv,
+    h_send, h_recv, x_send, x_recv, local, flushed, *refs,
 ):
     r, c = lax.axis_index("row"), lax.axis_index("col")
     tok, heads = q.shape
     width = x.shape[1]
+    half = n_col * width
+    n_unit = down_own.shape[0]
     rows = tok // N_CHUNK
     me = r * n_col + c
     row_base = r * n_col
-    greet(line_peers(r, c, n_col))
-    gather = LateGather(dy_full, ag_send, ag_recv, r, c, n_col, width)
-    scatter = Scatter(part, stage, inbox, rs_send, rs_recv, c, n_col)
+    sums = refs[0:1]
+    mine, far = span(r * n_unit, n_unit), span((1 - r) * n_unit, n_unit)
+    near_rows, far_rows = span(r * half, half), span((1 - r) * half, half)
+    block = span(me * width, width)
     everything = pl.ds(0, dy_full.shape[2])
-    flush = Flush(((heads_all, heads_out), (middle, middle_out), ((dy_full, everything), dy_out)), flushed, rows)
-
-    def block_load(source, block, sem):
-        return pltpu.make_async_copy(
-            source.reshape(N_CHUNK, rows, width), dy_full.at[:, :, span(block * width, width)], sem
-        )
-
-    own = block_load(dy, me, local.at[0])
-    own.start()
+
+    def chunk_rows(chunk):
+        return span(chunk * rows, rows)
+
+    scale_wide, grad_branch = seg_col, x
+    late = LateGather(dy_full, dy_send, dy_recv, r, c, n_col, width)
+    gather = Gather(full, ag_send, ag_recv, r, c, n_col, width)
+    scatter_z = Scatter(part, stage_z, inbox_z, z_send, z_recv, c, n_col)
+    scatter_f = Scatter(part, stage_f, inbox_f, f_send, f_recv, c, n_col)
+    totals = Totals(held, sent, arrived, t_send, t_recv, r, c)
+    flush = Flush(
+        (
+            ((full, near_rows), h2_out), (grad_gate, gate_out), (grad_up, up_out), (units, units_out),
+            (grad_middle, middle_grad_out), (grad_branch, branch_out),
+            (heads_all, heads_out), (middle, middle_out), ((dy_full, everything), dy_out),
+        ),
+        flushed, rows,
+    )
+    panels = []
+    if n_sum:
+
+        def tile(owner, side):
+            cols = half // 4
+            n_row = sums[0].shape[0]
+            right = dy_full[:, :, span(r * half + side * cols, cols)].reshape(tok, cols)
+            return dot_tn(units[:, span(owner * n_row, n_row)], right)
+
+        panels.append(Reduce(tile, sums, *refs[1:]))
+
+    def block_load(source, at):
+        return source.reshape(N_CHUNK, rows, width), dy_full.at[:, :, span(at * width, width)]
+
+    own, *first = fetches(
+        [block_load(dy, me), (q_in, q), (k_in, k), (v_in, v), (seg_col_in, seg_col), (wo, w_out), (x_in, x)],
+        local,
+    )
     early = [
-        block_load(dy_end, row_base + gather.near_end, local.at[1]),
-        block_load(dy_mid, row_base + gather.other, local.at[2]),
+        pltpu.make_async_copy(*block_load(dy_end, row_base + late.near_end), local.at[7]),
+        pltpu.make_async_copy(*block_load(dy_mid, row_base + late.other), local.at[8]),
     ]
 
-    @pl.when(jnp.logical_not(gather.end))
+    @pl.when(jnp.logical_not(late.end))
     def _():
         for copy in early:
             copy.start()
 
-    load = pltpu.make_async_copy(wo, w_out, local.at[3])
-    load.start()
+    greet(group_peers(r, c, n_col) + (square_peers() if n_sum else []))
+    loads = fetches(
+        [
+            (wg.at[:, mine], gate_own.at[near_rows, :]),
+            (wg_other, gate_own.at[far_rows, :]),
+            (wu.at[:, mine], up_own.at[near_rows, :]),
+            (wu_other, up_own.at[far_rows, :]),
+            (wd.at[mine, :], down_own.at[:, near_rows]),
+            (wd_other, down_own.at[:, far_rows]),
+            (wg.at[:, far], gate_far),
+            (wu.at[:, far], up_far),
+        ],
+        local.at[pl.ds(9, 8)],
+    )
     own.wait()
 
-    @pl.when(jnp.logical_not(gather.end))
+    @pl.when(jnp.logical_not(late.end))
     def _():
         for copy in early:
             copy.wait()
 
-    gather.start()
 
     def heads_copy(chunk):
         piece = heads_all.at[pl.ds(chunk * rows, rows), span(r * heads, heads)]
@@ -730,137 +801,23 @@
         )
         heads_all[at, span(r * heads, heads)] = total.astype(BF16)
         inv_sum[at, :] = inverse
+        heads_copy(chunk).start()
 
     def contract(chunk):
+        heads_copy(chunk).wait_recv()
+        flush.start(chunk, (6,))
         part[chunk] = dot_nn(heads_all[span(chunk * rows, rows), :], w_out[...])
-
-    for chunk in range(N_CHUNK):
-        attend(chunk)
-        heads_copy(chunk).start()
-        if chunk == 0:
-            load.wait()
-        if chunk >= 1:
-            scatter.near(chunk - 1)
-        if chunk >= 2:
-            scatter.far(chunk - 2)
-            gather.relay(chunk - 2)
-        heads_copy(chunk).wait_recv()
-        flush.start(chunk, (0,))
-        contract(chunk)
-        scatter.open(chunk)
-    gather.relay(N_CHUNK - 2)
-    gather.relay(N_CHUNK - 1)
-    scatter.near(N_CHUNK - 1)
-    scatter.far(N_CHUNK - 2)
-    gather.collect(0)
-    scatter.far(N_CHUNK - 1)
-
-    def settle(chunk, carry):
-        at = span(chunk * rows, rows)
-        scatter.total(chunk, middle, at)
-        middle[at, :] += x[at, :].astype(F32)
-        pl.when(chunk > 0)(lambda: gather.collect(chunk))
-        gather.inner.wait_other(chunk)
-        flush.start(chunk, (1, 2))
-        return carry
-
-    lax.fori_loop(0, N_CHUNK, settle, 0)
-    gather.finish()
-    scatter.finish()
-    for chunk in range(N_CHUNK):
-        heads_copy(chunk).wait_send()
-    flush.finish()
-
-
-def attend(n_col, q, k, v, seg_row, seg_col, x, wo, dy, dy_end, dy_mid):
-    tok, heads = q.shape
-    width = x.shape[1]
-    shape = jax.ShapeDtypeStruct
-    outs = [
-        shape((tok, 2 * heads), BF16),
-        shape((tok, 128), F32),
-        shape((tok, width), F32),
-        shape((tok, 2 * n_col * width), BF16),
-    ]
-    scratch = [
-        pltpu.VMEM((tok, 2 * heads), BF16),
-        pltpu.VMEM((tok, width), F32),
-        pltpu.VMEM((N_CHUNK, tok // N_CHUNK, 2 * n_col * width), BF16),
-        pltpu.VMEM(wo.shape, BF16),
-        *Scatter.scratch(n_col, tok // N_CHUNK, width),
-        *gather_sems(n_col),
-        pltpu.SemaphoreType.DMA((N_CHUNK,)),
-        pltpu.SemaphoreType.DMA((N_CHUNK,)),
-        pltpu.SemaphoreType.DMA((4,)),
-        pltpu.SemaphoreType.DMA((3, N_CHUNK)),
-    ]
-    return kernel_call(
-        functools.partial(attend_kernel, n_col), "attend", 2, outs, [True, False, True, True],
-        [vmem()] * 6 + [anywhere()] * 4, scratch, 8 * tok * tok * heads,
-    )(q, k, v, seg_row, seg_col, x, wo, dy, dy_end, dy_mid)
-
-
-def ffn_kernel(
-    n_col, n_sum,
-    middle, gain, dy_full, wg, wu, wd, wg_other, wu_other, wd_other,
-    h2_out, units_out, gate_out, up_out, middle_grad_out, branch_out, gain_sum, sum_out,
-    units, grad_gate, grad_up, grad_middle, grad_branch,
-    full, gate_own, up_own, down_own, gate_far, up_far, scale_wide, grad_two,
-    part, stage, inbox, rs_send, rs_recv, held, sent, arrived, st_send, st_recv,
-    ag_send, ag_recv, x_send, x_recv, local, flushed, *refs,
-):
-    r, c = lax.axis_index("row"), lax.axis_index("col")
-    tok, width = middle.shape
-    half = n_col * width
-    n_unit = down_own.shape[0]
-    rows = tok // N_CHUNK
-    me = r * n_col + c
-    sums = refs[0:1]
-
-    def chunk_rows(chunk):
-        return span(chunk * rows, rows)
-
-    gather = Gather(full, ag_send, ag_recv, r, c, n_col, width)
-    scatter = Scatter(part, stage, inbox, rs_send, rs_recv, c, n_col)
-    totals = Totals(held, sent, arrived, st_send, st_recv, r, c)
-    mine, far = span(r * n_unit, n_unit), span((1 - r) * n_unit, n_unit)
-    near_rows, far_rows = span(r * half, half), span((1 - r) * half, half)
-    flush = Flush(
-        (
-            ((full, near_rows), h2_out), (grad_gate, gate_out), (grad_up, up_out), (units, units_out),
-            (grad_middle, middle_grad_out), (grad_branch, branch_out),
-        ),
-        flushed, rows,
-    )
-    loads = [
-        pltpu.make_async_copy(src, dst, local.at[n])
-        for n, (src, dst) in enumerate(
-            (
-                (wg.at[:, mine], gate_own.at[near_rows, :]),
-                (wg_other, gate_own.at[far_rows, :]),
-                (wu.at[:, mine], up_own.at[near_rows, :]),
-                (wu_other, up_own.at[far_rows, :]),
-                (wd.at[mine, :], down_own.at[:, near_rows]),
-                (wd_other, down_own.at[:, far_rows]),
-                (wg.at[:, far], gate_far),
-                (wu.at[:, far], up_far),
-            )
-        )
-    ]
-    block = span(me * width, width)
-    for chunk in range(N_CHUNK):
-        values = middle[chunk * rows : (chunk + 1) * rows, :]
+        scatter_z.open(chunk)
+
+    def settle_z(chunk):
+        at = chunk_rows(chunk)
+        scatter_z.total(chunk, middle, at)
+        values = middle[at, :] + x[at, :].astype(F32)
+        middle[at, :] = values
         full[chunk, 0:rows, block] = (values * gain[...]).astype(BF16)
         put_notes(full, chunk, block, (as_row(jnp.sum(values * values, axis=1, keepdims=True)),))
-    panels = []
-    if n_sum:
-        tile = tile_of(units, dy_full, sums[0].shape[0], r * half, half // 2)
-        panels.append(Reduce(tile, sums, *refs[1:]))
-    greet(group_peers(r, c, n_col) + (square_peers() if n_sum else []))
-    gather.start(0)
-    gather.start(1)
-    for copy in loads:
-        copy.start()
+        gather.start(chunk)
+        flush.start(chunk, (7,))
 
     def exchange(n, chunk):
         piece = (grad_gate, grad_up, units)[n].at[chunk_rows(chunk), mine]
@@ -873,18 +830,18 @@
         scale = lax.rsqrt(as_column(square) * (1.0 / (2 * half)) + norm_eps)
         scale_wide[chunk_rows(chunk), :] = jnp.broadcast_to(scale, (rows, scale_wide.shape[1]))
 
-    tile = n_unit // 2
+    size = n_unit // 2
 
     def units_part(chunk, step):
         at = chunk_rows(chunk)
         scale = scale_wide[at, 0:1]
-        cols = span(step * tile, tile)
+        cols = span(step * size, size)
         gate = dot_nn(full[chunk, 0:rows, :], gate_own[:, cols]) * scale
         up = dot_nn(full[chunk, 0:rows, :], up_own[:, cols]) * scale
-        grad = dot_nt(dy_full[at, :], down_own[cols, :])
+        grad = dot_nt(dy_full[chunk], down_own[cols, :])
         sig = jax.nn.sigmoid(gate)
         act = gate * sig
-        put = span(r * n_unit + step * tile, tile)
+        put = span(r * n_unit + step * size, size)
         units[at, put] = (act * up).astype(BF16)
         grad = grad * scale
         grad_gate[at, put] = (grad * up * sig * (1.0 + gate * (1.0 - sig))).astype(BF16)
@@ -895,16 +852,17 @@
         part[chunk] = dot_nt(grad_gate[at, mine], gate_own[near_rows, :]) + dot_nt(
             grad_up[at, mine], up_own[near_rows, :]
         )
-        for n in range(3):
+        for n in range(2):
             exchange(n, chunk).wait_recv()
-        flush.start(chunk, (0, 1, 2, 3))
         part[chunk] += dot_nt(grad_gate[at, far], gate_far[...]) + dot_nt(grad_up[at, far], up_far[...])
-        scatter.open(chunk)
-
-    def settle(chunk):
+        scatter_f.open(chunk)
+        exchange(2, chunk).wait_recv()
+        flush.start(chunk, (0, 1, 2, 3, 8))
+
+    def settle_f(chunk):
         at = chunk_rows(chunk)
-        scatter.total(chunk, grad_two, at)
-        product = grad_two[at, :] * middle[at, :]
+        scatter_f.total(chunk, grad_middle, at)
+        product = grad_middle[at, :] * middle[at, :]
         totals.note(chunk, jnp.sum(product * gain[...], axis=1, keepdims=True))
         gain_sum[...] += jnp.sum(product.reshape(rows // 8, 8, width), axis=0)
 
@@ -913,49 +871,110 @@
         mean = totals.column(chunk) * (1.0 / (2 * half))
         scale = scale_wide[at, 0:1]
         grad = (
-            dy_full[at, span(me * width, width)].astype(F32)
-            + grad_two[at, :] * gain[...]
+            dy_full[chunk, :, block].astype(F32)
+            + grad_middle[at, :] * gain[...]
             - middle[at, :] * (scale * scale * mean)
         )
         grad_middle[at, :] = grad
         grad_branch[at, :] = grad.astype(BF16)
         flush.start(chunk, (4, 5))
 
+    middle_role = scatter_z.middle
+
+    def at_end(*acts):
+        @pl.when(jnp.logical_not(middle_role))
+        def _():
+            for act, *what in acts:
+                act(*what)
+
+    def at_middle(*acts):
+        @pl.when(middle_role)
+        def _():
+            for act, *what in acts:
+                act(*what)
+
+    near, far_sum = scatter_z.near, scatter_z.far
+    near_f, far_f = scatter_f.near, scatter_f.far
+    end_relay, middle_relay = gather.end_relay, gather.middle_relay
     gain_sum[...] = jnp.zeros_like(gain_sum)
-    gather.tick(0)
-    gather.start(2)
-    gather.tick(1)
-    gather.start(3)
-    gather.tick(2)
+    at_end(*[(late.start, chunk) for chunk in range(N_CHUNK)])
+    at_middle((late.start, 0), (late.start, 1), (late.start, 2))
+    for copy in first:
+        copy.wait()
+    at_middle((late.relay, 0), (late.start, 3))
+    attend(0)
+    contract(0)
+    at_middle((near, 0))
+    attend(1)
+    attend(2)
+    at_middle((far_sum, 0))
+    contract(1)
+    at_middle((near, 1), (far_sum, 1))
+    contract(2)
+    at_middle((near, 2), (far_sum, 2))
+    settle_z(0)
+    settle_z(1)
+    attend(3)
+    at_middle((middle_relay, "b", 0))
+    at_end((late.collect, 0))
+    at_middle((middle_relay, "a", 0), (middle_relay, "b", 1), (middle_relay, "c", 0))
+    settle_z(2)
+    at_middle((late.relay, 1), (middle_relay, "c", 1), (middle_relay, "a", 1), (middle_relay, "a", 2))
+    at_end((end_relay, 1, 0))
+    contract(3)
+    at_middle((near, 3), (middle_relay, "b", 2))
+    at_end((end_relay, 3, 0), (end_relay, 2, 0))
     for copy in loads:
         copy.wait()
 
     def step(now, carry):
-        @pl.when(now < N_CHUNK)
+        late.inner.wait_other(now)
+        gather.wait_other(now)
+        norm(now)
+
+        def part_step(n, carry):
+            units_part(now, n)
+            return carry
+
+        lax.fori_loop(0, 2, part_step, 0)
+        for n in range(3):
+            exchange(n, now).start()
+        pl.when(now == 1)(lambda: at_middle((near_f, 0), (middle_relay, "a", 3)))
+        pl.when(now == 3)(lambda: at_middle((far_f, 1), (near_f, 2), (far_f, 2)))
+        back(now)
+
+        @pl.when(now == 0)
         def _():
-            gather.wait_other(now)
-            norm(now)
-
-            def part_step(n, carry):
-                units_part(now, n)
-                return carry
-
-            lax.fori_loop(0, 2, part_step, 0)
-            for n in range(3):
-                exchange(n, now).start()
-
-        pl.when((now >= 1) & (now <= N_CHUNK))(lambda: scatter.near(now - 1))
-        pl.when((now >= 2) & (now <= N_CHUNK + 1))(lambda: scatter.far(now - 2))
-        pl.when(now < N_CHUNK)(lambda: back(now))
-        gather.tick(now + 3)
-        pl.when((now >= 3) & (now <= N_CHUNK + 2))(lambda: settle(now - 3))
-        for panel in panels:
-            pl.when(now == N_CHUNK - 1)(panel.first)
-            pl.when(now == N_CHUNK + 1)(panel.second)
-            pl.when(now == N_CHUNK + 1)(panel.merge)
+            at_end((end_relay, 2, 1), (end_relay, 1, 1))
+            at_middle((far_sum, 3))
+            settle_z(3)
+            at_middle((middle_relay, "c", 2), (late.relay, 2))
+            at_end((end_relay, 3, 1), (late.collect, 1))
+
+        @pl.when(now == 1)
+        def _():
+            at_middle((middle_relay, "b", 3), (late.relay, 3))
+            at_end((end_relay, 1, 2), (end_relay, 2, 2), (end_relay, 2, 3), (end_relay, 3, 2), (late.collect, 2))
+
+        @pl.when(now == 2)
+        def _():
+            at_middle((middle_relay, "c", 3), (far_f, 0), (near_f, 1))
+            at_end((end_relay, 3, 3), (end_relay, 1, 3), (late.collect, 3))
+
         return carry
 
-    lax.fori_loop(0, N_CHUNK + 3, step, 0)
+    lax.fori_loop(0, N_CHUNK, step, 0)
+    for panel in panels:
+        panel.first()
+    at_middle((near_f, 3), (far_f, 3))
+    for panel in panels:
+        panel.second()
+
+    def drain(now, carry):
+        settle_f(now)
+        return carry
+
+    lax.fori_loop(0, N_CHUNK, drain, 0)
     totals.exchange()
 
     def close_up(chunk, carry):
@@ -964,15 +983,19 @@
 
     lax.fori_loop(0, N_CHUNK, close_up, 0)
     gather.finish()
-    scatter.finish()
+    late.finish()
+    scatter_z.finish()
+    scatter_f.finish()
     totals.finish()
     stores = []
     for panel in panels:
+        panel.merge()
         panel.last()
-        stores += fetches([(sums[0], sum_out)], local.at[pl.ds(8, 1)])
+        stores += fetches([(sums[0], sum_out)], local.at[pl.ds(17, 1)])
         panel.finish()
 
     def close(chunk, carry):
+        heads_copy(chunk).wait_send()
         for n in range(3):
             exchange(n, chunk).wait_send()
         return carry
@@ -983,45 +1006,61 @@
     flush.finish()
 
 
-def ffn(n_col, n_dp, middle, gain, dy_full, wg, wu, wd, wg_other, wu_other, wd_other):
-    tok, width = middle.shape
+def layer(
+    n_col, n_dp, q, k, v, seg_row, seg_col, x, gain, wo, dy, dy_end, dy_mid,
+    wg, wu, wd, wg_other, wu_other, wd_other,
+):
+    tok, heads = q.shape
+    width = x.shape[1]
     half, n_unit = n_col * width, wg.shape[1] // 2
+    rows = tok // N_CHUNK
     shape = jax.ShapeDtypeStruct
-    outs = [
-        shape((tok, half), BF16),
-        shape((tok, 2 * n_unit), BF16), shape((tok, 2 * n_unit), BF16), shape((tok, 2 * n_unit), BF16),
-        shape((tok, width), F32), shape((tok, width), BF16), shape((8, width), F32),
-    ]
     n_sum = int(n_dp == 4)
     size = (wd.shape[0] // 4, half // 2) if n_sum else (8, 128)
-    outs.append(shape(size, F32))
-    rows = tok // N_CHUNK
+    outs = [
+        shape((tok, 2 * heads), BF16), shape((tok, 128), F32), shape((tok, width), F32),
+        shape((tok, 2 * half), BF16), shape((tok, half), BF16),
+        shape((tok, 2 * n_unit), BF16), shape((tok, 2 * n_unit), BF16), shape((tok, 2 * n_unit), BF16),
+        shape((tok, width), F32), shape((tok, width), BF16), shape((8, width), F32), shape(size, F32),
+    ]
+    scatter = Scatter.scratch(n_col, rows, width)
     scratch = [
+        *[pltpu.VMEM(array.shape, array.dtype) for array in (q, k, v, seg_col, x)],
+        pltpu.VMEM((tok, 2 * heads), BF16),
+        pltpu.VMEM((tok, width), F32),
+        pltpu.VMEM((N_CHUNK, rows, 2 * half), BF16),
+        pltpu.VMEM(wo.shape, BF16),
         *[pltpu.VMEM((tok, 2 * n_unit), BF16)] * 3,
         pltpu.VMEM((tok, width), F32),
-        pltpu.VMEM((tok, width), BF16),
         pltpu.VMEM((N_CHUNK, rows + N_NOTE, 2 * half), BF16),
         pltpu.VMEM((2 * half, n_unit), BF16),
         pltpu.VMEM((2 * half, n_unit), BF16),
         pltpu.VMEM((n_unit, 2 * half), BF16),
         pltpu.VMEM((half, n_unit), BF16),
         pltpu.VMEM((half, n_unit), BF16),
-        pltpu.VMEM((tok, 128), F32),
-        pltpu.VMEM((tok, width), F32),
-        *Scatter.scratch(n_col, rows, width),
+        *scatter,
+        *scatter[1:],
         *Totals.scratch(rows),
         *gather_sems(n_col),
+        *gather_sems(n_col),
+        pltpu.SemaphoreType.DMA((N_CHUNK,)),
+        pltpu.SemaphoreType.DMA((N_CHUNK,)),
         pltpu.SemaphoreType.DMA((3, N_CHUNK)),
         pltpu.SemaphoreType.DMA((3, N_CHUNK)),
-        pltpu.SemaphoreType.DMA((9,)),
-        pltpu.SemaphoreType.DMA((6, N_CHUNK)),
+        pltpu.SemaphoreType.DMA((18,)),
+        pltpu.SemaphoreType.DMA((9, N_CHUNK)),
     ]
     if n_sum:
         scratch += [pltpu.VMEM(size, F32), *Reduce.scratch(size[0], size[1] // 2)]
     return kernel_call(
-        functools.partial(ffn_kernel, n_col, n_sum), "ffn", 3, outs, [True] * 6 + [False, True],
-        [vmem()] * 3 + [anywhere()] * 6, scratch, 20 * tok * half * n_unit,
-    )(middle, gain, dy_full, wg, wu, wd, wg_other, wu_other, wd_other)
+        functools.partial(layer_kernel, n_col, n_sum), "layer", 2, outs,
+        [True, False, True, True] + [True] * 6 + [False, True],
+        [anywhere()] * 3 + [vmem(), anywhere(), anywhere(), vmem()] + [anywhere()] * 10,
+        scratch, 20 * tok * half * n_unit,
+    )(
+        q, k, v, seg_row, seg_col, x, gain, wo, dy, dy_end, dy_mid,
+        wg, wu, wd, wg_other, wu_other, wd_other,
+    )
 
 
 class Reduce:
@@ -1621,11 +1660,12 @@
         n_col, tokens, gain_one, positions, segments, grad_output,
         w_query, w_key, w_value, w_out, w_gate, w_up, w_down,
     )
-    heads_all, inv_sum, middle, dy_full = attend(
-        n_col, q, k, v, segments, seg_col, tokens, w_out, grad_output, dy_end, dy_mid
-    )
-    h2, units, grad_gate, grad_up, grad_middle, branch, gain_sum, down_one = ffn(
-        n_col, n_dp, middle, gain_two, dy_full, w_gate, w_up, w_down, wg_other, wu_other, wd_other
+    (
+        heads_all, inv_sum, middle, dy_full,
+        h2, units, grad_gate, grad_up, grad_middle, branch, gain_sum, down_one,
+    ) = layer(
+        n_col, n_dp, q, k, v, segments, seg_col, tokens, gain_two, w_out, grad_output, dy_end, dy_mid,
+        w_gate, w_up, w_down, wg_other, wu_other, wd_other,
     )
     output, grad_heads, branch_half, *sums_one = branch_back(
         n_col, n_dp, branch, units, w_down, middle, dy_full, h2, grad_gate, w_out, wo_other, heads_all

time: 351 us -> 334 us (0.952)
  Pallas kernels: 349 us -> 332 us
    pallas_call x2 -> x1, Pallas kernels: 146 us -> 128 us  [layer(): kernel_call(functools.partial(layer_kernel, n_col, n_sum), 'layer', 2, ou...]
where the time goes in v1:
time: 334 us; the launch traced here: 333 us
  Pallas kernels  332 us (99%)
    pallas_call x1, Pallas kernels, layer(): kernel_call(functools.partial(layer_kernel, n_col, n_sum), 'layer', 2, ou...  128 us
    pallas_call x1, Pallas kernels, attend_back(): kernel_call(functools.partial(attend_back_kernel, n_col, n_dp, n_sum), 'a...  77.5 us
    pallas_call x1, Pallas kernels, branch_back(): kernel_call(functools.partial(branch_kernel, n_col, n_sum), 'branch', 4,...  68 us
    pallas_call x1, Pallas kernels, project(): kernel_call(functools.partial(project_kernel, n_col), 'project', 1, outs,...  49.2 us
    pallas_call x1, Pallas kernels, finish(): pl.pallas_call(functools.partial(finish_kernel, groups, share), out_shape...  9.55 us

profile of v1, /device:TPU:0, one launch (start us, length us, event | category | flops | bytes accessed | tf_op | source)
XLA Modules:
  0.0 333.4 jit_solution(11291176176808661920)
XLA Ops:
  0.7 0.6 pad_maximum_fusion.rope
  1.2 49.2 %project.1 = (bf16[1024,256]{1,0:T(8,128)(2,1)}, bf16[1024,256]{1,0:T(8,128)(2,1)}, bf16[1024,256]{1,0:T(8,128)(2,1)}, bf16[1024,1024]{1,0:T(8,128)(2,1)}, f32[1...) custom-call(bf16[1024,256]{1,0:T(8,128)(2,1)} %x_in.3, ...), custom_call_target="tpu_custom_call" | custom-call | flops 3221225472 | bytes 16777216 | tf_op jit(solution)/shard_map/project/pallas_call | solution.py:609
  50.4 127.7 %layer.1 = (bf16[1024,512]{1,0:T(8,128)(2,1)}, f32[1024,128]{1,0:T(8,128)}, f32[1024,256]{1,0:T(8,128)}, bf16[1024,2048]{1,0:T(8,128)(2,1)}, bf16[1024,1024]{1,0...) custom-call(bf16[1024,256]{1,0:T(8,128)(2,1)} %get-tuple-element.59., ...), custom_call_target="tpu_custom_call" | custom-call | flops 21474836480 | bytes 16777216 | tf_op jit(solution)/shard_map/layer/pallas_call | solution.py:1055
  178.1 68.0 %branch.1 = (f32[1024,256]{1,0:T(8,128)}, bf16[1024,256]{1,0:T(8,128)(2,1)}, bf16[1024,1024]{1,0:T(8,128)(2,1)}, f32[512,512]{1,0:T(8,128)}, f32[256,2048]{1,0:T(8,128)}, /*index=5*/f32[128,1024]{1,0:T(8,128)}) custom-call(bf16[1024,256]{1,0:T(8,128)(2,1)} %get-tuple-element.68.branch, bf16[1024,2048]{1,0:T(8,128)(2,1)} %get-tuple-element.69.units_in, ...), custom_call_target="tpu_custom_call" | custom-call | flops 12884901888 | bytes 16777216 | tf_op jit(solution)/shard_map/branch/pallas_call | solution.py:1335
  246.2 77.5 %attend_back.1 = (f32[1024,256]{1,0:T(8,128)}, f32[2,8,256]{2,1,0:T(8,128)}, bf16[8,128]{1,0:T(8,128)(2,1)}, f32[256,2048]{1,0:T(8,128)}, f32[256,512]{1,0:T(8,1...) custom-call(bf16[1024,256]{1,0:T(8,128)(2,1)} %get-tuple-element.59.q_in, bf16[1024,256]{1,0:T(8,128)(2,1)} %get-tuple-element.60.k_in, ...), custom_call_target="tpu_custom_call" | custom-call | flops 4294967296 | bytes 16777216 | tf_op jit(solution)/shard_map/attend_back/pallas_call | solution.py:1574
  323.7 9.6 %finish.1 = (f32[1,64]{1,0:T(1,128)}, f32[1,64]{1,0:T(1,128)}, f32[1024,256]{1,0:T(8,128)}, f32[1024,256]{1,0:T(8,128)}, f32[256,512]{1,0:T(8,128)}, /*index=5*/...) custom-call(f32[2,8,256]{2,1,0:T(8,128)} %get-tuple-element.85.gain_, ...), custom_call_target="tpu_custom_call" | custom-call | tf_op jit(solution)/shard_map/finish/pallas_call | solution.py:1625
  (1 shorter events, 0.0 us)

commit v2 on v1

--- a/solution.py
+++ b/solution.py
@@ -2,6 +2,7 @@
 
 import jax
 import jax.numpy as jnp
+import numpy as np
 from jax import lax
 from jax.experimental import pallas as pl
 from jax.experimental.pallas import tpu as pltpu
@@ -347,13 +348,17 @@
             self.sent.at[step], self.inbox.at[step], self.send.at[step], self.recv.at[step], self.partners[step]
         )
 
+    def step(self, n):
+        if n > 0:
+            self.copy(n - 1).wait_recv()
+            self.held[...] += self.inbox[n - 1]
+        if n < 3:
+            self.sent[n] = self.held[...]
+            self.copy(n).start()
+
     def exchange(self):
-        for step in range(3):
-            self.sent[step] = self.held[...]
-            copy = self.copy(step)
-            copy.start()
-            copy.wait_recv()
-            self.held[...] += self.inbox[step]
+        for n in range(4):
+            self.step(n)
 
     def column(self, chunk):
         return as_column(self.held[pl.ds(chunk, 1), :])
@@ -471,12 +476,16 @@
         local,
     )
     mine = span(me * width, width)
-    for chunk in range(N_CHUNK):
-        values = x[chunk * rows : (chunk + 1) * rows, :]
+
+    def prepare(chunk, carry):
+        values = x[span(chunk * rows, rows), :]
         full[chunk, 0:rows, mine] = values
         values = values.astype(F32)
         square = as_row(jnp.sum(values * values, axis=1, keepdims=True))
         put_notes(full, chunk, mine, (square, gain[...]))
+        return carry
+
+    lax.fori_loop(0, N_CHUNK, prepare, 0)
     greet(group_peers(r, c, n_col))
     gather = Gather(full, ag_send, ag_recv, r, c, n_col, width)
     flush = Flush(((q, q_out), (k, k_out), (v, v_out), (h1, h1_out)), flushed, rows)
@@ -580,9 +589,9 @@
     full = 2 * n_col * width
     half = n_col * width
     heads, units = wq.shape[1] // 2, wg.shape[1] // 2
-    lane = jnp.arange(128) % HD
-    inv_freq = rope_base ** (-2.0 * (lane % (HD // 2)).astype(F32) / HD)
-    rope = jnp.stack([inv_freq, jnp.where(lane < HD // 2, -1.0, 1.0)])
+    lane = np.arange(128) % HD
+    inv_freq = rope_base ** (-2.0 * (lane % (HD // 2)) / HD)
+    rope = jnp.asarray(np.stack([inv_freq, np.where(lane < HD // 2, -1.0, 1.0)]), F32)
     shape = jax.ShapeDtypeStruct
     outs = [
         shape((tok, heads), BF16), shape((tok, heads), BF16), shape((tok, heads), BF16),
@@ -688,12 +697,12 @@
     q_in, k_in, v_in, seg_row, seg_col_in, x_in, gain, wo, dy, dy_end, dy_mid,
     wg, wu, wd, wg_other, wu_other, wd_other,
     heads_out, inv_sum, middle_out, dy_out,
-    h2_out, units_out, gate_out, up_out, middle_grad_out, branch_out, gain_sum, sum_out,
+    h2_out, units_out, gate_out, up_out, two_out, scale_out, gain_sum, held, sum_out,
     q, k, v, seg_col, x, heads_all, middle, dy_full, w_out,
-    units, grad_gate, grad_up, grad_middle,
+    units, grad_gate, grad_up, grad_two,
     full, gate_own, up_own, down_own, gate_far, up_far,
     part, stage_z, inbox_z, z_send, z_recv, stage_f, inbox_f, f_send, f_recv,
-    held, sent, arrived, t_send, t_recv, dy_send, dy_recv, ag_send, ag_recv,
+    dy_send, dy_recv, ag_send, ag_recv,
     h_send, h_recv, x_send, x_recv, local, flushed, *refs,
 ):
     r, c = lax.axis_index("row"), lax.axis_index("col")
@@ -713,16 +722,15 @@
     def chunk_rows(chunk):
         return span(chunk * rows, rows)
 
-    scale_wide, grad_branch = seg_col, x
+    scale_wide = seg_col
     late = LateGather(dy_full, dy_send, dy_recv, r, c, n_col, width)
     gather = Gather(full, ag_send, ag_recv, r, c, n_col, width)
     scatter_z = Scatter(part, stage_z, inbox_z, z_send, z_recv, c, n_col)
     scatter_f = Scatter(part, stage_f, inbox_f, f_send, f_recv, c, n_col)
-    totals = Totals(held, sent, arrived, t_send, t_recv, r, c)
     flush = Flush(
         (
             ((full, near_rows), h2_out), (grad_gate, gate_out), (grad_up, up_out), (units, units_out),
-            (grad_middle, middle_grad_out), (grad_branch, branch_out),
+            (grad_two, two_out), (scale_wide, scale_out),
             (heads_all, heads_out), (middle, middle_out), ((dy_full, everything), dy_out),
         ),
         flushed, rows,
@@ -755,7 +763,7 @@
         for copy in early:
             copy.start()
 
-    greet(group_peers(r, c, n_col) + (square_peers() if n_sum else []))
+    greet(line_peers(r, c, n_col) + (square_peers() if n_sum else []))
     loads = fetches(
         [
             (wg.at[:, mine], gate_own.at[near_rows, :]),
@@ -857,27 +865,15 @@
         part[chunk] += dot_nt(grad_gate[at, far], gate_far[...]) + dot_nt(grad_up[at, far], up_far[...])
         scatter_f.open(chunk)
         exchange(2, chunk).wait_recv()
-        flush.start(chunk, (0, 1, 2, 3, 8))
+        flush.start(chunk, (0, 1, 2, 3, 5, 8))
 
     def settle_f(chunk):
         at = chunk_rows(chunk)
-        scatter_f.total(chunk, grad_middle, at)
-        product = grad_middle[at, :] * middle[at, :]
-        totals.note(chunk, jnp.sum(product * gain[...], axis=1, keepdims=True))
+        scatter_f.total(chunk, grad_two, at)
+        product = grad_two[at, :] * middle[at, :]
+        held[pl.ds(chunk, 1), :] = as_row(jnp.sum(product * gain[...], axis=1, keepdims=True))
         gain_sum[...] += jnp.sum(product.reshape(rows // 8, 8, width), axis=0)
-
-    def conclude(chunk):
-        at = chunk_rows(chunk)
-        mean = totals.column(chunk) * (1.0 / (2 * half))
-        scale = scale_wide[at, 0:1]
-        grad = (
-            dy_full[chunk, :, block].astype(F32)
-            + grad_middle[at, :] * gain[...]
-            - middle[at, :] * (scale * scale * mean)
-        )
-        grad_middle[at, :] = grad
-        grad_branch[at, :] = grad.astype(BF16)
-        flush.start(chunk, (4, 5))
+        flush.start(chunk, (4,))
 
     middle_role = scatter_z.middle
 
@@ -897,6 +893,7 @@
     near_f, far_f = scatter_f.near, scatter_f.far
     end_relay, middle_relay = gather.end_relay, gather.middle_relay
     gain_sum[...] = jnp.zeros_like(gain_sum)
+    held[...] = jnp.zeros_like(held)
     at_end(*[(late.start, chunk) for chunk in range(N_CHUNK)])
     at_middle((late.start, 0), (late.start, 1), (late.start, 2))
     for copy in first:
@@ -912,8 +909,12 @@
     at_middle((near, 1), (far_sum, 1))
     contract(2)
     at_middle((near, 2), (far_sum, 2))
-    settle_z(0)
-    settle_z(1)
+
+    def settle_first(chunk, carry):
+        settle_z(chunk)
+        return carry
+
+    lax.fori_loop(0, 2, settle_first, 0)
     attend(3)
     at_middle((middle_relay, "b", 0))
     at_end((late.collect, 0))
@@ -975,18 +976,10 @@
         return carry
 
     lax.fori_loop(0, N_CHUNK, drain, 0)
-    totals.exchange()
-
-    def close_up(chunk, carry):
-        conclude(chunk)
-        return carry
-
-    lax.fori_loop(0, N_CHUNK, close_up, 0)
     gather.finish()
     late.finish()
     scatter_z.finish()
     scatter_f.finish()
-    totals.finish()
     stores = []
     for panel in panels:
         panel.merge()
@@ -1021,7 +1014,8 @@
         shape((tok, 2 * heads), BF16), shape((tok, 128), F32), shape((tok, width), F32),
         shape((tok, 2 * half), BF16), shape((tok, half), BF16),
         shape((tok, 2 * n_unit), BF16), shape((tok, 2 * n_unit), BF16), shape((tok, 2 * n_unit), BF16),
-        shape((tok, width), F32), shape((tok, width), BF16), shape((8, width), F32), shape(size, F32),
+        shape((tok, width), F32), shape((tok, 128), F32), shape((8, width), F32), shape((8, rows), F32),
+        shape(size, F32),
     ]
     scatter = Scatter.scratch(n_col, rows, width)
     scratch = [
@@ -1040,7 +1034,6 @@
         pltpu.VMEM((half, n_unit), BF16),
         *scatter,
         *scatter[1:],
-        *Totals.scratch(rows),
         *gather_sems(n_col),
         *gather_sems(n_col),
         pltpu.SemaphoreType.DMA((N_CHUNK,)),
@@ -1054,7 +1047,7 @@
         scratch += [pltpu.VMEM(size, F32), *Reduce.scratch(size[0], size[1] // 2)]
     return kernel_call(
         functools.partial(layer_kernel, n_col, n_sum), "layer", 2, outs,
-        [True, False, True, True] + [True] * 6 + [False, True],
+        [True, False, True, True] + [True] * 6 + [False, False, True],
         [anywhere()] * 3 + [vmem(), anywhere(), anywhere(), vmem()] + [anywhere()] * 10,
         scratch, 20 * tok * half * n_unit,
     )(
@@ -1166,6 +1159,13 @@
     return [(always, {"dp": y * 2 + 1 - x}), (always, {"dp": (1 - y) * 2 + x})]
 
 
+def pick(step, table):
+    value = jnp.int32(table[0])
+    for n in range(1, len(table)):
+        value = jnp.where(step == n, table[n], value)
+    return value
+
+
 def tile_of(left, right, n_row, base=0, width=None):
     cols = (right.shape[1] if width is None else width) // 2
 
@@ -1175,17 +1175,22 @@
     return tile
 
 
+def far_peers(c):
+    return [(c >= 0, {"col": c + 2 - 4 * (c // 2)})]
+
+
 def branch_kernel(
     n_col, n_sum,
-    branch, units_in, wd, middle_in, dy_full, h2_in, gate_in, wo, wo_other, heads_in,
+    two_in, scale_in, sums_in, gain, units_in, wd, middle_in, dy_full, h2_in, gate_in, wo, wo_other, heads_in,
     *refs,
 ):
-    (output_out, heads_out, half_out), refs = refs[:3], refs[3:]
+    (output_out, heads_out, half_out, middle_grad_out), refs = refs[:4], refs[4:]
     sums_out, refs = refs[:n_sum], refs[n_sum:]
     (
-        units, middle, h2, grad_gate, heads_all, branch_half, output, grad_heads,
-        full, down, dy_half, w_out, part, stage, inbox, rs_send, rs_recv, ag_send, ag_recv, local, flushed,
-    ), refs = refs[:21], refs[21:]
+        units, middle, h2, grad_gate, heads_all, branch_half, output, grad_heads, grad_middle, scale_wide,
+        full, down, dy_half, w_out, part, stage, inbox, rs_send, rs_recv,
+        held, sent, arrived, t_send, t_recv, ag_send, ag_recv, local, flushed,
+    ), refs = refs[:28], refs[28:]
     sums, refs = refs[:n_sum], refs[n_sum:]
     r, c = lax.axis_index("row"), lax.axis_index("col")
     tok, width = middle.shape
@@ -1193,119 +1198,182 @@
     heads = grad_heads.shape[1]
     rows = tok // N_CHUNK
     me = r * n_col + c
-    mine, other = span(r * half, half), span((1 - r) * half, half)
-    own, dy_load, units_load, down_load, *loads = fetches(
+    mine, other, block = span(r * half, half), span((1 - r) * half, half), span(me * width, width)
+    copies = fetches(
         [
-            (branch.reshape(N_CHUNK, rows, width), full.at[:, :, span(me * width, width)]),
-            (dy_full.at[:, mine], dy_half),
-            (units_in, units),
-            (wd, down),
-            (h2_in, h2),
-            (gate_in, grad_gate),
-            (wo.at[span(r * heads, heads), :], w_out.at[:, mine]),
-            (wo_other, w_out.at[:, other]),
-            (middle_in, middle),
+            (dy_full.at[:, mine], dy_half), (units_in, units), (two_in, grad_middle), (middle_in, middle),
+            (scale_in, scale_wide), (wd, down), (h2_in, h2), (gate_in, grad_gate),
+            (wo.at[span(r * heads, heads), :], w_out.at[:, mine]), (wo_other, w_out.at[:, other]),
             (heads_in, heads_all),
         ],
         local,
     )
-    greet(line_peers(r, c, n_col) + (square_peers() if n_sum else []))
+    totals = Totals(held, sent, arrived, t_send, t_recv, r, c)
+    held[...] = sums_in[...]
+    greet(line_peers(r, c, n_col) + far_peers(c) + (square_peers() if n_sum else []))
+    totals.step(0)
     gather = Gather(full, ag_send, ag_recv, r, c, n_col, width)
     scatter = Scatter(part, stage, inbox, rs_send, rs_recv, c, n_col)
-    flush = Flush(((output, output_out), (grad_heads, heads_out), (branch_half, half_out)), flushed, rows)
-    own.wait()
-
-    def begin_gather(chunk, carry):
-        gather.start(chunk)
-        return carry
-
-    lax.fori_loop(0, N_CHUNK, begin_gather, 0)
+    flush = Flush(
+        ((output, output_out), (grad_heads, heads_out), (branch_half, half_out), (grad_middle, middle_grad_out)),
+        flushed, rows,
+    )
     panels = []
     if n_sum:
         terms = ((units, dy_half, half // 2, half // 2), (h2, grad_gate, 0, None), (heads_all, branch_half, 0, None))
         for n, (left, right, base, cols) in enumerate(terms):
             tile = tile_of(left, right, sums[n].shape[0], base, cols)
             panels.append(Reduce(tile, (sums[n],), *refs[6 * n : 6 * n + 6]))
-    dy_load.wait()
-    units_load.wait()
-    for panel in panels[:1]:
-        panel.first()
-    down_load.wait()
-
-    def begin(chunk, carry):
+
+    def panel_do(n, *whats):
+        if n_sum:
+            for what in whats:
+                getattr(panels[n], what)()
+
+    def at_end(*acts):
+        @pl.when(jnp.logical_not(scatter.middle))
+        def _():
+            for distance, chunk in acts:
+                gather.end_relay(distance, chunk)
+
+    def at_middle(*acts):
+        @pl.when(scatter.middle)
+        def _():
+            for act, *what in acts:
+                act(*what)
+
+    def conclude(chunk):
+        at = span(chunk * rows, rows)
+        mean = totals.column(chunk) * (1.0 / (2 * half))
+        scale = scale_wide[at, 0:1]
+        grad = (
+            dy_half[at, span(c * width, width)].astype(F32)
+            + grad_middle[at, :] * gain[...]
+            - middle[at, :] * (scale * scale * mean)
+        )
+        grad_middle[at, :] = grad
+        full[chunk, :, block] = grad.astype(BF16)
+        gather.start(chunk)
+        flush.start(chunk, (3,))
+
+    def outward(chunk):
         part[chunk] = dot_nn(units[span(chunk * rows, rows), :], down[...])
         scatter.open(chunk)
-        gather.relay(1, chunk)
-        return carry
-
-    lax.fori_loop(0, N_CHUNK, begin, 0)
-    for copy in loads:
-        copy.wait()
-    for panel in panels[1:2]:
-        panel.first()
-
-    def carry_on(chunk, carry):
-        gather.relay(2, chunk)
-        scatter.near(chunk)
-        return carry
-
-    lax.fori_loop(0, N_CHUNK, carry_on, 0)
-    for panel in panels[:1]:
-        panel.second()
-
-    def arrive(chunk, carry):
-        gather.relay(3, chunk)
-        scatter.far(chunk)
-        return carry
-
-    lax.fori_loop(0, N_CHUNK, arrive, 0)
-
-    def copy_half(chunk, carry):
+
+    def heads_back(chunk):
+        at = span(chunk * rows, rows)
         gather.wait_other(chunk)
-        branch_half[span(chunk * rows, rows), :] = full[chunk, :, mine]
-        return carry
-
-    lax.fori_loop(0, N_CHUNK, copy_half, 0)
-    for panel in panels[2:]:
-        panel.first()
-    for panel in panels[:1]:
-        panel.merge()
-    for panel in panels[1:2]:
-        panel.second()
-
-    def settle(chunk, carry):
+        branch_half[at, :] = full[chunk, :, mine]
+        grad_heads[at, :] = dot_nt(full[chunk], w_out[...]).astype(BF16)
+        flush.start(chunk, (1, 2))
+
+    def settle(chunk):
         at = span(chunk * rows, rows)
-        grad_heads[at, :] = dot_nt(full[chunk], w_out[...]).astype(BF16)
         scatter.total(chunk, output, at)
         output[at, :] += middle[at, :]
-        flush.start(chunk)
+        flush.start(chunk, (0,))
+
+    relay, near, far = gather.middle_relay, scatter.near, scatter.far
+    totals.step(1)
+    for copy in copies[:2]:
+        copy.wait()
+    panel_do(0, "first")
+    totals.step(2)
+    for copy in copies[2:6]:
+        copy.wait()
+    def store(n):
+        return pltpu.make_async_copy(sums[n], sums_out[n], local.at[11 + n])
+
+    def stored(n):
+        if n_sum:
+            store(n).start()
+
+    def after_first():
+        for copy in copies[6:]:
+            copy.wait()
+        panel_do(1, "first")
+        totals.step(3)
+
+        def one(step, carry):
+            conclude(pick(step, (1, 2, 0, 3)))
+            return carry
+
+        lax.fori_loop(0, N_CHUNK, one, 0)
+        at_middle((relay, "a", 2), (relay, "a", 0), (relay, "b", 1), (relay, "b", 2), (relay, "c", 1))
+        at_end((2, 2))
+        at_middle((relay, "b", 3), (relay, "a", 1), (near, 3))
+
+    def after_third():
+        at_middle((relay, "c", 3), (relay, "b", 0), (far, 3))
+        at_end((2, 1), (3, 1), (2, 0), (1, 2), (1, 1))
+        panel_do(1, "second")
+
+    def after_fifth():
+        panel_do(1, "merge")
+        panel_do(0, "second")
+        at_end((3, 2))
+        at_middle((near, 2), (far, 0))
+
+    def after_sixth():
+        panel_do(1, "last")
+        stored(1)
+        at_end((1, 0), (3, 3), (3, 0))
+        at_middle((far, 2))
+
+    def after_seventh():
+        at_middle((near, 1))
+        at_end((2, 3), (1, 3))
+
+    def stage(now, carry):
+        turn = pick(now, (0, 0, 0, 1, 0, 1, 1, 1))
+        chunk = pick(now, (3, 0, 2, 1, 1, 2, 0, 3))
+        pl.when(turn == 0)(lambda: outward(chunk))
+        pl.when(turn == 1)(lambda: heads_back(chunk))
+        pl.when(now == 0)(after_first)
+        pl.when(now == 1)(lambda: at_middle((relay, "a", 3)))
+        pl.when(now == 2)(after_third)
+        pl.when(now == 3)(lambda: at_middle((relay, "c", 2), (near, 0), (relay, "c", 0)))
+        pl.when(now == 4)(after_fifth)
+        pl.when(now == 5)(after_sixth)
+        pl.when(now == 6)(after_seventh)
         return carry
 
-    lax.fori_loop(0, N_CHUNK, settle, 0)
-    for panel in panels[1:2]:
-        panel.merge()
-    for panel in panels[2:]:
-        panel.second()
-        panel.merge()
-    stores = []
-    for n, panel in enumerate(panels):
-        panel.last()
-        stores += fetches([(sums[n], sums_out[n])], local.at[pl.ds(10 + n, 1)])
+    lax.fori_loop(0, 8, stage, 0)
+    panel_do(2, "first")
+
+    def before_last():
+        panel_do(2, "second")
+        panel_do(0, "merge", "last")
+        stored(0)
+
+    def close_up(now, carry):
+        pl.when(now == 1)(lambda: at_middle((far, 1)))
+        pl.when(now == 3)(before_last)
+        settle(pick(now, (2, 0, 3, 1)))
+        return carry
+
+    lax.fori_loop(0, N_CHUNK, close_up, 0)
+    panel_do(2, "merge", "last")
+    stored(2)
     gather.finish()
     scatter.finish()
-    for panel in panels:
+    totals.finish()
+    for n, panel in enumerate(panels):
         panel.finish()
-    for copy in stores:
-        copy.wait()
+        store(n).wait()
     flush.finish()
 
 
-def branch_back(n_col, n_dp, branch, units, wd, middle, dy_full, h2, grad_gate, wo, wo_other, heads_all):
+def branch_back(
+    n_col, n_dp, two, scale, held, gain, units, wd, middle, dy_full, h2, grad_gate, wo, wo_other, heads_all
+):
     tok, width = middle.shape
     half, heads = n_col * width, wo_other.shape[0]
     rows = tok // N_CHUNK
     shape = jax.ShapeDtypeStruct
-    outs = [shape((tok, width), F32), shape((tok, heads), BF16), shape((tok, half), BF16)]
+    outs = [
+        shape((tok, width), F32), shape((tok, heads), BF16), shape((tok, half), BF16), shape((tok, width), F32)
+    ]
     scratch = [
         pltpu.VMEM(units.shape, BF16),
         pltpu.VMEM(middle.shape, F32),
@@ -1315,14 +1383,17 @@
         pltpu.VMEM((tok, half), BF16),
         pltpu.VMEM((tok, width), F32),
         pltpu.VMEM((tok, heads), BF16),
+        pltpu.VMEM((tok, width), F32),
+        pltpu.VMEM(scale.shape, F32),
         pltpu.VMEM((N_CHUNK, rows, 2 * half), BF16),
         pltpu.VMEM(wd.shape, BF16),
         pltpu.VMEM((tok, half), BF16),
         pltpu.VMEM((heads, 2 * half), BF16),
         *Scatter.scratch(n_col, rows, width),
+        *Totals.scratch(rows),
         *gather_sems(n_col),
-        pltpu.SemaphoreType.DMA((13,)),
-        pltpu.SemaphoreType.DMA((3, N_CHUNK)),
+        pltpu.SemaphoreType.DMA((14,)),
+        pltpu.SemaphoreType.DMA((4, N_CHUNK)),
     ]
     n_sum = 0
     if n_dp == 4:
@@ -1334,8 +1405,8 @@
             scratch += Reduce.scratch(size[0], size[1] // 2)
     return kernel_call(
         functools.partial(branch_kernel, n_col, n_sum), "branch", 4, outs, [True] * len(outs),
-        [anywhere()] * 10, scratch, 12 * tok * half * half,
-    )(branch, units, wd, middle, dy_full, h2, grad_gate, wo, wo_other, heads_all)
+        [anywhere(), anywhere(), vmem(), vmem()] + [anywhere()] * 9, scratch, 12 * tok * half * half,
+    )(two, scale, held, gain, units, wd, middle, dy_full, h2, grad_gate, wo, wo_other, heads_all)
 
 
 def attend_back_kernel(
@@ -1469,35 +1540,36 @@
     attend(last)
     for copy in later:
         copy.wait()
+    contract(last)
     attend(last - 1)
-    contract(last)
     panel_do(0, "second")
-    attend(last - 2)
     contract(last - 1)
     scatter.near(last)
+    attend(last - 2)
     attend(last - 3)
     contract(last - 2)
     scatter.near(last - 1)
     scatter.far(last)
     contract(last - 3)
     panel_do(1, "first")
-    scatter.near(last - 2)
     scatter.far(last - 1)
     panel_do(0, "merge")
     settle(last)
+    panel_do(0, "last")
+    scatter.near(last - 2)
     scatter.near(last - 3)
     scatter.far(last - 2)
     panel_do(1, "second")
+    scatter.far(last - 3)
 
     def settle_step(now, carry):
-        pl.when(now == 1)(lambda: scatter.far(0))
-        settle(last - now)
+        settle(pick(now, (last - 2, last - 1, last - 3)))
+        pl.when(now == 0)(lambda: panel_do(1, "merge"))
         return carry
 
-    lax.fori_loop(1, N_CHUNK, settle_step, 0)
+    lax.fori_loop(0, 3, settle_step, 0)
     gain_box[d] = gain_mine[...]
     others(lambda at: gain_copy(at).start())
-    panel_do(1, "merge")
     totals.exchange()
 
     def close_up(step, carry):
@@ -1512,8 +1584,8 @@
     gain_sums[...] = gain_total
     stores = []
     where = len(copies)
+    panel_do(1, "last")
     for n, panel in enumerate(panels):
-        panel.last()
         for m in range(1, n_sum) if n else range(1):
             stores += fetches([(sums[m], sums_out[m])], local.at[pl.ds(where + m, 1)])
     if not n_sum:
@@ -1662,13 +1734,14 @@
     )
     (
         heads_all, inv_sum, middle, dy_full,
-        h2, units, grad_gate, grad_up, grad_middle, branch, gain_sum, down_one,
+        h2, units, grad_gate, grad_up, grad_two, scale, gain_sum, held, down_one,
     ) = layer(
         n_col, n_dp, q, k, v, segments, seg_col, tokens, gain_two, w_out, grad_output, dy_end, dy_mid,
         w_gate, w_up, w_down, wg_other, wu_other, wd_other,
     )
-    output, grad_heads, branch_half, *sums_one = branch_back(
-        n_col, n_dp, branch, units, w_down, middle, dy_full, h2, grad_gate, w_out, wo_other, heads_all
+    output, grad_heads, branch_half, grad_middle, *sums_one = branch_back(
+        n_col, n_dp, grad_two, scale, held, gain_two, units, w_down, middle, dy_full, h2, grad_gate,
+        w_out, wo_other, heads_all,
     )
     grad_tokens, gain_sums, triple, *sums_two = attend_back(
         n_col, n_dp, q, k, v, grad_heads, segments, seg_col, inv_sum, cos_table, sin_table, tokens, r1,

time: 334 us -> 323 us (0.967)
  Pallas kernels: 332 us -> 322 us
    pallas_call x1, Pallas kernels: 77.5 us -> 68.9 us  [attend_back(): kernel_call(functools.partial(attend_back_kernel, n_col, n_dp, n_sum), 'a...]
where the time goes in v2:
time: 323 us
  Pallas kernels  322 us (100%)
    pallas_call x1, Pallas kernels, layer(): kernel_call(functools.partial(layer_kernel, n_col, n_sum), 'layer', 2, ou...  124 us
    pallas_call x1, Pallas kernels, branch_back(): kernel_call(functools.partial(branch_kernel, n_col, n_sum), 'branch', 4,...  69.5 us
    pallas_call x1, Pallas kernels, attend_back(): kernel_call(functools.partial(attend_back_kernel, n_col, n_dp, n_sum), 'a...  68.9 us
    pallas_call x1, Pallas kernels, project(): kernel_call(functools.partial(project_kernel, n_col), 'project', 1, outs,...  49.5 us
    pallas_call x1, Pallas kernels, finish(): pl.pallas_call(functools.partial(finish_kernel, groups, share), out_shape...  9.55 us

profile of v2, /device:TPU:0, one launch (start us, length us, event | category | flops | bytes accessed | tf_op | source)
XLA Modules:
  0.0 322.7 jit_solution(2876750150459632981)
XLA Ops:
  0.6 49.5 %project.1 = (bf16[1024,256]{1,0:T(8,128)(2,1)}, bf16[1024,256]{1,0:T(8,128)(2,1)}, bf16[1024,256]{1,0:T(8,128)(2,1)}, bf16[1024,1024]{1,0:T(8,128)(2,1)}, f32[1...) custom-call(bf16[1024,256]{1,0:T(8,128)(2,1)} %x_in.3, ...), custom_call_target="tpu_custom_call" | custom-call | flops 3221225472 | bytes 16777216 | tf_op jit(solution)/shard_map/project/pallas_call | solution.py:618
  50.1 124.5 %layer.1 = (bf16[1024,512]{1,0:T(8,128)(2,1)}, f32[1024,128]{1,0:T(8,128)}, f32[1024,256]{1,0:T(8,128)}, bf16[1024,2048]{1,0:T(8,128)(2,1)}, bf16[1024,1024]{1,0...) custom-call(bf16[1024,256]{1,0:T(8,128)(2,1)} %get-tuple-element.61., ...), custom_call_target="tpu_custom_call" | custom-call | flops 21474836480 | bytes 16777216 | tf_op jit(solution)/shard_map/layer/pallas_call | solution.py:1048
  174.6 69.5 %branch.1 = (f32[1024,256]{1,0:T(8,128)}, bf16[1024,256]{1,0:T(8,128)(2,1)}, bf16[1024,1024]{1,0:T(8,128)(2,1)}, f32[1024,256]{1,0:T(8,128)}, f32[512,512]{1,0:T...) custom-call(f32[1024,256]{1,0:T(8,128)} %get-tuple-element.70.two_in, f32[1024,128]{1,0:T(8,128)} %get-tuple-element.71.scale_in, ...), custom_call_target="tpu_custom_call" | custom-call | flops 12884901888 | bytes 16777216 | tf_op jit(solution)/shard_map/branch/pallas_call | solution.py:1406
  244.1 68.9 %attend_back.1 = (f32[1024,256]{1,0:T(8,128)}, f32[2,8,256]{2,1,0:T(8,128)}, bf16[8,128]{1,0:T(8,128)(2,1)}, f32[256,2048]{1,0:T(8,128)}, f32[256,512]{1,0:T(8,1...) custom-call(bf16[1024,256]{1,0:T(8,128)(2,1)} %get-tuple-element.61.q_in, bf16[1024,256]{1,0:T(8,128)(2,1)} %get-tuple-element.62.k_in, ...), custom_call_target="tpu_custom_call" | custom-call | flops 4294967296 | bytes 16777216 | tf_op jit(solution)/shard_map/attend_back/pallas_call | solution.py:1646
  313.0 9.6 %finish.1 = (f32[1,64]{1,0:T(1,128)}, f32[1,64]{1,0:T(1,128)}, f32[1024,256]{1,0:T(8,128)}, f32[1024,256]{1,0:T(8,128)}, f32[256,512]{1,0:T(8,128)}, /*index=5*/...) custom-call(f32[2,8,256]{2,1,0:T(8,128)} %get-tuple-element.89.gain_, ...), custom_call_target="tpu_custom_call" | custom-call | tf_op jit(solution)/shard_map/finish/pallas_call | solution.py:1697

commit v3 on v2

--- a/solution.py
+++ b/solution.py
@@ -1664,14 +1664,10 @@
     for result, parts in zip(results, groups):
         cols = result.shape[1] // parts
         targets += [result.at[:, pl.ds(part * cols, cols)] for part in range(parts)]
-    pieces = 2
     inward, outward = [], []
     for n, (source, keep, target) in enumerate(zip(sources, held, targets)):
-        rows = keep.shape[0] // pieces
-        for piece in range(pieces):
-            at = pl.ds(piece * rows, rows)
-            inward.append(pltpu.make_async_copy(source.at[at, :], keep.at[at, :], get.at[n, piece]))
-            outward.append(pltpu.make_async_copy(keep.at[at, :], target.at[at, :], put.at[n, piece]))
+        inward.append(pltpu.make_async_copy(source, keep, get.at[n]))
+        outward.append(pltpu.make_async_copy(keep, target, put.at[n]))
     for copy in inward:
         copy.start()
     d = lax.axis_index("dp")
@@ -1700,7 +1696,7 @@
         in_specs=[vmem()] + [anywhere()] * n_copy,
         out_specs=[vmem()] * 2 + [anywhere()] * len(arrays),
         scratch_shapes=[pltpu.VMEM(x.shape, x.dtype) for x in flat]
-        + [pltpu.SemaphoreType.DMA((n_copy, 2)), pltpu.SemaphoreType.DMA((n_copy, 2))],
+        + [pltpu.SemaphoreType.DMA((n_copy,)), pltpu.SemaphoreType.DMA((n_copy,))],
         compiler_params=pltpu.CompilerParams(vmem_limit_bytes=VMEM_LIMIT),
         name="finish",
     )(gain_sums, *flat)

time: 323 us -> 322 us (level)
  no operation moved by 1% of the time
where the time goes in v3:
time: 322 us
  Pallas kernels  321 us (100%)
    pallas_call x1, Pallas kernels, layer(): kernel_call(functools.partial(layer_kernel, n_col, n_sum), 'layer', 2, ou...  124 us
    pallas_call x1, Pallas kernels, branch_back(): kernel_call(functools.partial(branch_kernel, n_col, n_sum), 'branch', 4,...  69.5 us
    pallas_call x1, Pallas kernels, attend_back(): kernel_call(functools.partial(attend_back_kernel, n_col, n_dp, n_sum), 'a...  68.9 us
    pallas_call x1, Pallas kernels, project(): kernel_call(functools.partial(project_kernel, n_col), 'project', 1, outs,...  49.5 us
    pallas_call x1, Pallas kernels, finish(): pl.pallas_call(functools.partial(finish_kernel, groups, share), out_shape...  8.47 us

profile of v3, /device:TPU:0, one launch (start us, length us, event | category | flops | bytes accessed | tf_op | source)
XLA Modules:
  0.0 321.7 jit_solution(7280067860574582624)
XLA Ops:
  0.6 49.5 %project.1 = (bf16[1024,256]{1,0:T(8,128)(2,1)}, bf16[1024,256]{1,0:T(8,128)(2,1)}, bf16[1024,256]{1,0:T(8,128)(2,1)}, bf16[1024,1024]{1,0:T(8,128)(2,1)}, f32[1...) custom-call(bf16[1024,256]{1,0:T(8,128)(2,1)} %x_in.3, ...), custom_call_target="tpu_custom_call" | custom-call | flops 3221225472 | bytes 16777216 | tf_op jit(solution)/shard_map/project/pallas_call | solution.py:618
  50.1 124.5 %layer.1 = (bf16[1024,512]{1,0:T(8,128)(2,1)}, f32[1024,128]{1,0:T(8,128)}, f32[1024,256]{1,0:T(8,128)}, bf16[1024,2048]{1,0:T(8,128)(2,1)}, bf16[1024,1024]{1,0...) custom-call(bf16[1024,256]{1,0:T(8,128)(2,1)} %get-tuple-element.61., ...), custom_call_target="tpu_custom_call" | custom-call | flops 21474836480 | bytes 16777216 | tf_op jit(solution)/shard_map/layer/pallas_call | solution.py:1048
  174.6 69.5 %branch.1 = (f32[1024,256]{1,0:T(8,128)}, bf16[1024,256]{1,0:T(8,128)(2,1)}, bf16[1024,1024]{1,0:T(8,128)(2,1)}, f32[1024,256]{1,0:T(8,128)}, f32[512,512]{1,0:T...) custom-call(f32[1024,256]{1,0:T(8,128)} %get-tuple-element.70.two_in, f32[1024,128]{1,0:T(8,128)} %get-tuple-element.71.scale_in, ...), custom_call_target="tpu_custom_call" | custom-call | flops 12884901888 | bytes 16777216 | tf_op jit(solution)/shard_map/branch/pallas_call | solution.py:1406
  244.1 68.9 %attend_back.1 = (f32[1024,256]{1,0:T(8,128)}, f32[2,8,256]{2,1,0:T(8,128)}, bf16[8,128]{1,0:T(8,128)(2,1)}, f32[256,2048]{1,0:T(8,128)}, f32[256,512]{1,0:T(8,1...) custom-call(bf16[1024,256]{1,0:T(8,128)(2,1)} %get-tuple-element.61.q_in, bf16[1024,256]{1,0:T(8,128)(2,1)} %get-tuple-element.62.k_in, ...), custom_call_target="tpu_custom_call" | custom-call | flops 4294967296 | bytes 16777216 | tf_op jit(solution)/shard_map/attend_back/pallas_call | solution.py:1646
  313.0 8.5 %finish.1 = (f32[1,64]{1,0:T(1,128)}, f32[1,64]{1,0:T(1,128)}, f32[1024,256]{1,0:T(8,128)}, f32[1024,256]{1,0:T(8,128)}, f32[256,512]{1,0:T(8,128)}, /*index=5*/...) custom-call(f32[2,8,256]{2,1,0:T(8,128)} %get-tuple-element.89.gain_, ...), custom_call_target="tpu_custom_call" | custom-call | tf_op jit(solution)/shard_map/finish/pallas_call | solution.py:1693
